TPU v7x, 128 devices: a whole 4x4x4 slice. The times are simulated.
128 devices in a mesh: dp: 32 (over y, z, core), mp: 4 (over x).
Axes of the slice: x: 4, y: 4, z: 4, core: 2. Of those that a mesh axis runs over, the one named last changes fastest.
Arguments:
- gradients: bfloat16 [4, 16, 1024, 1024], P(None, 'mp', 'dp'), as said below
- statistics: float32 [4, 32, 1024, 1024], P('mp', 'dp'), as said below
- accumulator: float32 [4, 16, 1024, 1024], P(None, 'mp', 'dp'), may hold values from 0.25 to 4
Outputs:
- update: float32 [4, 16, 1024, 1024], P(None, 'mp', 'dp')
- statistics_new: float32 [4, 32, 1024, 1024], P('mp', 'dp')
- accumulator_new: float32 [4, 16, 1024, 1024], P(None, 'mp', 'dp')
Inputs may be any that keep to these rules, and one draw needn't show every extreme that they name: `gradients`: Real-valued gradient blocks. `statistics`: each 1024 x 1024 statistic is symmetric positive definite.
All inputs are finite; a program needn't handle non-finite values.
Results may differ from a plain program's by a relative error of at most 0.005.
The roundings to bfloat16 on the way count: a program that leaves them out, or rounds other values in their place, can miss the bound.
Values may be sent and summed in bfloat16 or wider, within the bound.
A program may use at most 64 MiB of HBM per device.

v0:
```python
import functools

import jax
import jax.numpy as jnp
from jax import lax
from jax.sharding import Mesh
from jax.sharding import PartitionSpec as P

ITERS = 3
DP = ("dp_0", "dp_1", "dp_2")
DP_MP = ("dp_0", "dp_1", "dp_2", "mp")


def one_axis_at_a_time(value, axes):
    return functools.reduce(lax.psum, axes, value)


def split_up(value, dim, size):
    before, after = (value.shape[:dim], value.shape[dim + 1 :])
    return jnp.moveaxis(value.reshape(*before, size, -1, *after), dim, 0)


def joined_along(parts, dim):
    parts = jnp.moveaxis(parts, 0, dim)
    dims = parts.shape
    return parts.reshape(*dims[:dim], dims[dim] * dims[dim + 1], *dims[dim + 2 :])


def moved_by_axis(parts, axes, sequence):
    inside = parts.shape[1:]
    result = parts.reshape(*(lax.axis_size(a) for a in axes), *inside)
    for k in sequence:
        result = lax.all_to_all(result, axes[k], k, k, tiled=True)
    return result.reshape(-1, *inside)


def exchange_by_chip(value, groups, sequence, split_dim, concat_dim):
    size = lax.axis_size(groups[0]) * lax.axis_size(groups[1])
    parts = split_up(value, split_dim, size)
    return joined_along(moved_by_axis(parts, groups, sequence), concat_dim)


def partner_2(value, axis, distance):
    return lax.ppermute(value, axis, [(i, i ^ 1 << distance) for i in range(lax.axis_size(axis))])


def batch_dot(left, right):
    return jnp.einsum("kij,kjl->kil", left, right, preferred_element_type=jnp.float32)


def inverse_roots(statistic):
    block_width = statistic.shape[-1]
    identity = jnp.eye(block_width, dtype=jnp.float32)
    frob_norms = jnp.sqrt(jnp.sum(statistic * statistic, axis=(1, 2)) + 1e-06)
    newton_scale = (2.5 / frob_norms)[:, None, None]
    matrix = newton_scale * statistic
    root_iter = jnp.sqrt(jnp.sqrt(newton_scale)) * identity
    for iteration in range(ITERS):
        factor = (1.25 * identity - 0.25 * matrix).astype(jnp.bfloat16)
        root_iter = batch_dot(root_iter.astype(jnp.bfloat16), factor)
        if iteration + 1 < ITERS:
            square = batch_dot(factor, factor).astype(jnp.bfloat16)
            fourth = batch_dot(square, square).astype(jnp.bfloat16)
            matrix = batch_dot(fourth, matrix.astype(jnp.bfloat16))
    return root_iter


def on_device(gradients, statistics, accumulator):
    owners = lax.axis_size(DP)
    own_index = lax.axis_index(DP)
    row_blocks, col_blocks, dev_rows, block_width = gradients.shape
    blocks = row_blocks * col_blocks
    owned_factors = statistics.shape[1]
    split_pairs = owned_factors == 1
    half_rows = dev_rows // 2
    parity = own_index % 2
    left_side = parity == 0
    by_block = gradients.reshape(blocks, dev_rows, block_width)
    grads_wide = gradients.astype(jnp.float32)
    grad_total = one_axis_at_a_time(jnp.sum(grads_wide * grads_wide), DP_MP)
    entries = blocks * dev_rows * block_width * owners * lax.axis_size("mp")
    clip_factor = jnp.minimum(1.0, jnp.sqrt(entries / (grad_total + 1e-06)))
    scaled = clip_factor * grads_wide
    accumulated = accumulator + scaled * scaled
    graft_step = scaled / jnp.sqrt(accumulated)
    graft_squares = jnp.sum(graft_step * graft_step)
    graft_total = one_axis_at_a_time(graft_squares, DP_MP)
    row_parts = 2
    row_units = by_block.reshape(blocks * row_parts, dev_rows // row_parts, block_width)
    received = exchange_by_chip(row_units, (("dp_0", "dp_1"), "dp_2"), (1, 0), 0, 1)
    partner_part = partner_2(received, DP, 0)
    own_part = received.reshape(owners, 1, half_rows, block_width)
    partner_part = partner_part.reshape(owners, 1, half_rows, block_width)
    ordered = jnp.where(
        left_side,
        jnp.concatenate([own_part, partner_part], 1),
        jnp.concatenate([partner_part, own_part], 1),
    )
    whole_blocks = ordered.reshape(1, owners * dev_rows, block_width)
    transposed = jnp.swapaxes(whole_blocks, 1, 2)
    factor_inputs = jnp.where(left_side, whole_blocks, transposed)
    gram_matrix = jnp.einsum(
        "kij,klj->kil", factor_inputs, factor_inputs, preferred_element_type=jnp.float32
    )
    statistics_new = (
        0.9 * statistics[0] + 0.1 / block_width * clip_factor * clip_factor * gram_matrix
    )
    root_values = inverse_roots(statistics_new).astype(jnp.bfloat16)
    partner = partner_2(root_values, DP, 0)
    left_root = jnp.where(left_side, root_values, partner)[0]
    right_root = jnp.where(left_side, partner, root_values)[0]
    left_rows = lax.dynamic_slice_in_dim(
        left_root.reshape(owners, 2, half_rows, block_width), parity, 1, 1
    )
    left_rows = left_rows.reshape(owners * half_rows, block_width)
    left_applied = jnp.dot(left_rows, whole_blocks[0], preferred_element_type=jnp.float32).astype(
        jnp.bfloat16
    )
    product = jnp.dot(left_applied, right_root, preferred_element_type=jnp.float32)
    pieces = product.reshape(1, owners, half_rows, block_width)
    update_total = one_axis_at_a_time(jnp.sum(product * product), DP_MP)
    returned = lax.all_to_all(
        pieces.astype(jnp.bfloat16), DP, split_axis=1, concat_axis=0, tiled=True
    ).astype(pieces.dtype)
    returned = returned.reshape(row_blocks, col_blocks, dev_rows, block_width)
    graft_ratio = jnp.sqrt(graft_total / (update_total + 1e-06))
    return (graft_ratio * returned, statistics_new[None], accumulated)


def solution(mesh):
    finer = Mesh(mesh.devices.reshape(4, 4, 2, mesh.shape["mp"]), ("dp_0", "dp_1", "dp_2", "mp"))
    in_specs = (P(None, "mp", DP, None), P("mp", DP, None, None), P(None, "mp", DP, None))
    out_specs = (P(None, "mp", DP, None), P("mp", DP, None, None), P(None, "mp", DP, None))
    return jax.shard_map(
        on_device, mesh=finer, in_specs=in_specs, out_specs=out_specs, check_vma=False
    )
```

profile of v0, /device:TPU:1, one launch (start us, length us, event | category | flops | bytes accessed | tf_op | source)
XLA Modules:
  0.0 190.4 jit_solution(14613944410347291302)
XLA Ops:
  0.6 1.3 copy.17
  2.0 5.6 %all_to_all.19 = bf16[16,2,1,16,1024]{4,3,0,2,1:T(8,128)(2,1)S(1)} all-to-all(bf16[16,2,1,16,1024]{4,3,0,2,1:T(8,128)(2,1)S(1)} %copy.17), channel_id=1, replica_groups=mesh['dp_0'=4,'dp_1'=4,'dp_2'=2,'mp'=4] {'dp_2'}, dimensions={1} | all-to-all | bytes 2097152 | tf_op jit(solution)/shard_map/all_to_all | solution.py:33
  7.5 0.0 copy-start
  7.5 0.1 copy.18
  7.7 23.8 %all_to_all.20 = bf16[16,2,1,16,1024]{4,3,1,2,0:T(8,128)(2,1)S(1)} all-to-all(bf16[16,2,1,16,1024]{4,3,1,2,0:T(8,128)(2,1)S(1)} %copy.18), channel_id=1, replica_groups=mesh['dp_0'=4,'dp_1'=4,'dp_2'=2,'mp'=4] {'dp_0','dp_1'}, dimensions={0} | all-to-all | bytes 2097152 | tf_op jit(solution)/shard_map/all_to_all | solution.py:33
  31.5 2.1 %collective-permute-start = (bf16[1,512,1024]{2,1,0:T(8,128)(2,1)S(1)}, bf16[1,512,1024]{2,1,0:T(8,128)(2,1)S(1)}, u32[]{:S(2)}, u32[]{:S(2)}) collective-permute-start(bf16[1,512,1024]{2,1,0:T(8,128)(2,1)S(1)} %bitcast.46), channel_id=1, source_target_pairs={{0,4},{4,0},{8,12},{12,8},{16,20},{20,16},{24,28},{28,24},{32,36},... | collective-permute-start | bytes 3145736 | tf_op jit(solution)/shard_map/ppermute | solution.py:44
  33.5 0.0 copy-done
  33.5 1.1 fusion.8
  34.7 7.4 %psum.84 = f32[]{:T(128)} all-reduce(f32[]{:T(128)} %fusion.8), channel_id=1, replica_groups=mesh['dp_0'=4,'dp_1'=4,'dp_2'=2,'mp'=4] {'dp_0'}, use_global_device_ids=true, to_apply=%region_1.2 | all-reduce | flops 1 | bytes 8 | tf_op jit(solution)/shard_map/psum | solution.py:15
  42.1 6.9 %psum.85 = f32[]{:T(128)} all-reduce(f32[]{:T(128)} %psum.84), channel_id=1, replica_groups=mesh['dp_0'=4,'dp_1'=4,'dp_2'=2,'mp'=4] {'dp_1'}, use_global_device_ids=true, to_apply=%region_2.3 | all-reduce | flops 1 | bytes 8 | tf_op jit(solution)/shard_map/psum | solution.py:15
  49.0 6.8 %psum.86 = f32[]{:T(128)} all-reduce(f32[]{:T(128)} %psum.85), channel_id=1, replica_groups=mesh['dp_0'=4,'dp_1'=4,'dp_2'=2,'mp'=4] {'dp_2'}, use_global_device_ids=true, to_apply=%region_3.4 | all-reduce | flops 1 | bytes 8 | tf_op jit(solution)/shard_map/psum | solution.py:15
  55.8 9.1 %psum.87 = f32[]{:T(128)} all-reduce(f32[]{:T(128)} %psum.86), channel_id=1, replica_groups=mesh['dp_0'=4,'dp_1'=4,'dp_2'=2,'mp'=4] {'mp'}, use_global_device_ids=true, to_apply=%region_4.5 | all-reduce | flops 1 | bytes 8 | tf_op jit(solution)/shard_map/psum | solution.py:15
  65.6 0.0 collective-permute-done
  65.6 0.3 maximum_select_fusion
  66.0 0.3 copy.19
  66.3 2.6 %copy.20 = bf16[1,1024,1024]{1,2,0:T(8,128)(2,1)} copy(bf16[1,1024,1024]{2,1,0:T(8,128)(2,1)S(1)} %bitcast.42) | data formatting | bytes 4194304 | tf_op jit(solution)/shard_map/jit(_where)/select_n | solution.py:94
  68.9 8.5 %multiply_reduce_fusion = (f32[]{:T(128)}, f32[1024,1024]{1,0:T(8,128)}) fusion(bf16[1,1024,1024]{2,1,0:T(8,128)(2,1)S(1)} %bitcast.43, bf16[1,1024,1024]{1,2,0:T(8,128)(2,1)} %copy.20, pred[]{:T(512)S(6)} %eq.16, f32[]{:T(128)S(6)} %mul.110, f32[1,1,1024,1024]{3,2,1,0:T(8,128)} %param.4), kind=kOutput, calls=%fused_computation.8 | convolution fusion | flops 2153775104 | bytes 12582921 | tf_op jit(solution)/shard_map/kij,klj->kil/dot_general | solution.py:102
  78.1 0.0 copy-start.1
  78.1 7.3 %fusion.60 = bf16[1024,1024]{1,0:T(8,128)(2,1)} fusion(f32[1024,1024]{1,0:T(8,128)} %get-tuple-element.16, f32[]{:T(128)S(6)} %div.14), kind=kOutput, calls=%fused_computation.57 | convolution fusion | flops 2153775104 | bytes 6291460 | tf_op jit(solution)/shard_map/kij,kjl->kil/dot_general | solution.py:48
  85.5 0.0 copy-done.1
  85.5 3.7 %fusion.10 = bf16[1024,1024]{1,0:T(8,128)(2,1)} fusion(bf16[]{:T(256)S(6)} %sqrt.30, f32[1024,1024]{1,0:T(8,128)S(1)} %copy-done.1, f32[]{:T(128)S(6)} %div.14), kind=kOutput, calls=%fused_computation.20 | convolution fusion | flops 2155872256 | bytes 6291462 | tf_op jit(solution)/shard_map/kij,kjl->kil/dot_general | solution.py:48
  89.2 9.9 %fusion.9 = f32[1024,1024]{1,0:T(8,128)} fusion(f32[1024,1024]{1,0:T(8,128)} %get-tuple-element.16, f32[]{:T(128)S(6)} %div.14, bf16[1024,1024]{1,0:T(8,128)(2,1)} %fusion.60), kind=kOutput, calls=%fused_computation.19 | convolution fusion | flops 4298113024 | bytes 10485764 | tf_op jit(solution)/shard_map/kij,kjl->kil/dot_general | solution.py:48
  99.1 14.2 %fusion.18 = bf16[1024,1024]{1,0:T(8,128)(2,1)} fusion(f32[1024,1024]{1,0:T(8,128)} %fusion.9), kind=kOutput, calls=%fused_computation.33 | convolution fusion | flops 4301258752 | bytes 6291456 | tf_op jit(solution)/shard_map/kij,kjl->kil/dot_general | solution.py:48
  113.2 6.5 %fusion.2 = bf16[1024,1024]{1,0:T(8,128)(2,1)} fusion(f32[1024,1024]{1,0:T(8,128)} %fusion.9, bf16[1024,1024]{1,0:T(8,128)(2,1)} %fusion.18), kind=kOutput, calls=%fused_computation.5 | convolution fusion | flops 2153775104 | bytes 8388608 | tf_op jit(solution)/shard_map/kij,kjl->kil/dot_general | solution.py:48
  119.7 9.3 %convert_bitcast_fusion = bf16[1,1024,1024]{2,1,0:T(8,128)(2,1)} fusion(bf16[1024,1024]{1,0:T(8,128)(2,1)} %fusion.2, bf16[1024,1024]{1,0:T(8,128)(2,1)} %fusion.10, f32[1024,1024]{1,0:T(8,128)} %fusion.9), kind=kOutput, calls=%fused_computation.30 | convolution fusion | flops 4302307328 | bytes 10485760 | tf_op jit(solution)/shard_map/kij,kjl->kil/dot_general | solution.py:48
  129.0 2.4 %collective-permute-start.1 = (bf16[1,1024,1024]{2,1,0:T(8,128)(2,1)}, bf16[1,1024,1024]{2,1,0:T(8,128)(2,1)}, u32[]{:S(2)}, u32[]{:S(2)}) collective-permute-start(bf16[1,1024,1024]{2,1,0:T(8,128)(2,1)} %convert_bitcast_fusion), channel_id=1, source_target_pairs={{0,4},{4,0},{8,12},{12,8},{16,20},{20,16},{24,28},{28,24},{32,36},... | collective-permute-start | bytes 6291464 | tf_op jit(solution)/shard_map/ppermute | solution.py:44
  131.4 4.1 %collective-permute-done.1 = bf16[1,1024,1024]{2,1,0:T(8,128)(2,1)} collective-permute-done((bf16[1,1024,1024]{2,1,0:T(8,128)(2,1)}, bf16[1,1024,1024]{2,1,0:T(8,128)(2,1)}, u32[]{:S(2)}, u32[]{:S(2)}) %collective-permute-start.1) | collective-permute-done | bytes 2097184 | tf_op jit(solution)/shard_map/ppermute | solution.py:44
  135.5 1.8 broadcast_select_fusion
  137.3 1.1 constant_dynamic-slice_fusion
  138.4 5.8 %multiply_reduce_fusion.1 = (f32[]{:T(128)}, bf16[512,1024]{1,0:T(8,128)(2,1)}) fusion(bf16[1,1024,1024]{2,1,0:T(8,128)(2,1)} %collective-permute-done.1, bf16[1,1024,1024]{2,1,0:T(8,128)(2,1)} %convert_bitcast_fusion, pred[]{:T(512)S(6)} %eq.16, bf16[512,1024]{1,0:T(8,128)(2,1)} %bitcast.50, bf16[1024,1024]{1,0:T(8,128)(2,1)S(1)} %bitcast.44), kind=kOutput, calls=%fused_computation.28 | convolution fusion | flops 2150629376 | bytes 8388613 | tf_op jit(solution)/shard_map/dot_general | solution.py:119
  144.2 4.0 %all-to-all-start.2 = ((bf16[1,32,16,1024]{3,2,0,1:T(8,128)(2,1)}), bf16[1,32,16,1024]{3,2,0,1:T(8,128)(2,1)S(1)}, u32[]{:S(2)}, u32[]{:S(2)}) async-start(bf16[1,32,16,1024]{3,2,0,1:T(8,128)(2,1)} %bitcast.51), calls=%async_computation.2 | async-start | bytes 2097152 | tf_op jit(solution)/shard_map/all_to_all | solution.py:122
  148.2 4.1 %fusion.7 = (f32[]{:T(128)}, f32[4,4,32,1024]{3,2,1,0:T(8,128)}) fusion(bf16[4,4,32,1024]{3,2,1,0:T(8,128)(2,1)S(1)} %copy-done, f32[]{:T(128)S(6)} %min_shard_map.3, f32[4,4,32,1024]{3,2,1,0:T(8,128)} %param.5), kind=kLoop, calls=%fused_computation.17 | loop fusion | flops 3670015 | bytes 5242888 | tf_op jit(solution)/shard_map/reduce_sum | solution.py:86
  152.2 12.9 %all-reduce.2 = (f32[]{:T(128)}, f32[]{:T(128)}) all-reduce(f32[]{:T(128)} %get-tuple-element.11, f32[]{:T(128)} %get-tuple-element.13), channel_id=1, replica_groups=mesh['dp_0'=4,'dp_1'=4,'dp_2'=2,'mp'=4] {'dp_0'}, use_global_device_ids=true, to_apply=%region_6.7 | all-reduce | flops 2 | bytes 16 | tf_op jit(solution)/shard_map/psum | solution.py:15
  165.1 9.0 %all-reduce.1 = (f32[]{:T(128)}, f32[]{:T(128)}) all-reduce(f32[]{:T(128)} %get-tuple-element.7, f32[]{:T(128)} %get-tuple-element.8), channel_id=1, replica_groups=mesh['dp_0'=4,'dp_1'=4,'dp_2'=2,'mp'=4] {'dp_1'}, use_global_device_ids=true, to_apply=%region_7.8 | all-reduce | flops 2 | bytes 16 | tf_op jit(solution)/shard_map/psum | solution.py:15
  174.1 6.7 %all-reduce.3 = (f32[]{:T(128)}, f32[]{:T(128)}) all-reduce(f32[]{:T(128)} %get-tuple-element.5, f32[]{:T(128)} %get-tuple-element.6), channel_id=1, replica_groups=mesh['dp_0'=4,'dp_1'=4,'dp_2'=2,'mp'=4] {'dp_2'}, use_global_device_ids=true, to_apply=%region_8.9 | all-reduce | flops 2 | bytes 16 | tf_op jit(solution)/shard_map/psum | solution.py:15
  180.8 6.7 %all-reduce = (f32[]{:T(128)}, f32[]{:T(128)}) all-reduce(f32[]{:T(128)} %get-tuple-element.9, f32[]{:T(128)} %get-tuple-element.10), channel_id=1, replica_groups=mesh['dp_0'=4,'dp_1'=4,'dp_2'=2,'mp'=4] {'mp'}, use_global_device_ids=true, to_apply=%region_9.10 | all-reduce | flops 2 | bytes 16 | tf_op jit(solution)/shard_map/psum | solution.py:15
  188.8 0.0 all-to-all-done.2
  188.8 1.6 convert_multiply_fusion.2
Async XLA Ops:
  7.5 26.0 %copy-start = (bf16[4,4,32,1024]{3,2,1,0:T(8,128)(2,1)S(1)}, bf16[4,4,32,1024]{3,2,1,0:T(8,128)(2,1)}, u32[]{:S(2)}) copy-start(bf16[4,4,32,1024]{3,2,1,0:T(8,128)(2,1)} %param.3) | copy-start | bytes 3145732
  31.5 34.2 %collective-permute-start = (bf16[1,512,1024]{2,1,0:T(8,128)(2,1)S(1)}, bf16[1,512,1024]{2,1,0:T(8,128)(2,1)S(1)}, u32[]{:S(2)}, u32[]{:S(2)}) collective-permute-start(bf16[1,512,1024]{2,1,0:T(8,128)(2,1)S(1)} %bitcast.46), channel_id=1, source_target_pairs={{0,4},{4,0},{8,12},{12,8},{16,20},{20,16},{24,28},{28,24},{32,36},... | collective-permute-start | bytes 3145736 | tf_op jit(solution)/shard_map/ppermute | solution.py:44
  78.1 7.3 %copy-start.1 = (f32[1024,1024]{1,0:T(8,128)S(1)}, f32[1024,1024]{1,0:T(8,128)}, u32[]{:S(2)}) copy-start(f32[1024,1024]{1,0:T(8,128)} %get-tuple-element.16) | copy-start | bytes 12582916
  129.0 6.5 %collective-permute-start.1 = (bf16[1,1024,1024]{2,1,0:T(8,128)(2,1)}, bf16[1,1024,1024]{2,1,0:T(8,128)(2,1)}, u32[]{:S(2)}, u32[]{:S(2)}) collective-permute-start(bf16[1,1024,1024]{2,1,0:T(8,128)(2,1)} %convert_bitcast_fusion), channel_id=1, source_target_pairs={{0,4},{4,0},{8,12},{12,8},{16,20},{20,16},{24,28},{28,24},{32,36},... | collective-permute-start | bytes 6291464 | tf_op jit(solution)/shard_map/ppermute | solution.py:44
  144.2 44.6 %all-to-all-start.2 = ((bf16[1,32,16,1024]{3,2,0,1:T(8,128)(2,1)}), bf16[1,32,16,1024]{3,2,0,1:T(8,128)(2,1)S(1)}, u32[]{:S(2)}, u32[]{:S(2)}) async-start(bf16[1,32,16,1024]{3,2,0,1:T(8,128)(2,1)} %bitcast.51), calls=%async_computation.2 | async-start | bytes 2097152 | tf_op jit(solution)/shard_map/all_to_all | solution.py:122
where the time goes:
time: 192 us; the launch traced here: 190 us
  blocking collectives  94.9 us (49%)
  matrix products  65.2 us (34%)
  other arithmetic  8.96 us (5%)
  starting transfers between devices  8.4 us (4%)
  local copies, waits for them, and re-layouts  5.35 us (3%)
  waiting for transfers between devices  4.13 us (2%)
  between operations  3.49 us (2%)
    psum x8, blocking collectives, one_axis_at_a_time(): return functools.reduce(lax.psum, axes, value)  65.5 us
    dot_general x6, matrix products, batch_dot(): jnp.einsum('kij,kjl->kil', left, right, preferred_element_type=jnp.float32)  50.9 us
    all_to_all x2, blocking collectives, moved_by_axis(): result = lax.all_to_all(result, axes[k], k, k, tiled=True)  29.4 us
    dot_general x1, matrix products, on_device(): jnp.einsum('kij,klj->kil', factor_inputs, factor_inputs, preferred_elemen...  8.49 us
    dot_general x1, matrix products, on_device(): jnp.dot(left_applied, right_root, preferred_element_type=jnp.float32)  5.81 us
    ppermute x2, starting transfers between devices, partner_2(): lax.ppermute(value, axis, [(i, i ^ 1 << distance) for i in range(lax.axis...  4.44 us
    ppermute x2, waiting for transfers between devices, partner_2(): lax.ppermute(value, axis, [(i, i ^ 1 << distance) for i in range(lax.axis...  4.13 us
    reduce_sum x1, other arithmetic, on_device(): graft_squares = jnp.sum(graft_step * graft_step)  4.07 us
  transfers between devices with their start and end apart: 3, of which 1 were waited for; matrix products, arithmetic and copies ran while one was open for 3% of the time, Pallas kernels for 0%

commit v1 on v0

v1 whole, which is shorter than its diff:
```python
import functools

import jax
import jax.numpy as jnp
from jax import lax
from jax.experimental import pallas as pl
from jax.experimental.pallas import tpu as pltpu
from jax.sharding import Mesh
from jax.sharding import PartitionSpec as P

F32 = jnp.float32
BF16 = jnp.bfloat16
MESH = pl.DeviceIdType.MESH
VMEM = pl.BlockSpec(memory_space=pltpu.VMEM)
ANY = pl.BlockSpec(memory_space=pl.ANY)

B = 1024
TILE = 256
NT = B // TILE
ROWS = 32
CHIPS = 16
ENTRIES = 4 * 16 * 1024 * 1024


def ring_distance(offset):
    return sum(min(step, 4 - step) for step in offset)


PLANE = sorted(
    [(dy, dz) for dy in range(4) for dz in range(4) if (dy, dz) != (0, 0)],
    key=lambda offset: -ring_distance(offset),
)
COLUMN = [(dx, dc) for dx in range(4) for dc in range(2) if (dx, dc) != (0, 0)]


class Place:
    def __init__(self):
        self.y, self.z, self.c, self.x = (lax.axis_index(a) for a in ("y", "z", "c", "mp"))
        self.chip = self.y * 4 + self.z
        self.column = self.x * 2 + self.c
        self.partner = {"c": 1 - self.c}

    def plane(self, offset):
        return {"y": lax.rem(self.y + offset[0], 4), "z": lax.rem(self.z + offset[1], 4)}

    def plane_chip(self, offset):
        return lax.rem(self.y + offset[0], 4) * 4 + lax.rem(self.z + offset[1], 4)

    def plane_source(self, offset):
        return lax.rem(self.y + 4 - offset[0], 4) * 4 + lax.rem(self.z + 4 - offset[1], 4)

    def in_column(self, offset):
        return {"mp": lax.rem(self.x + offset[0], 4), "c": lax.rem(self.c + offset[1], 2)}

    def greet(self):
        barrier = pltpu.get_barrier_semaphore()
        for offset in PLANE:
            pl.semaphore_signal(barrier, 1, device_id=self.plane(offset), device_id_type=MESH)
        for offset in COLUMN:
            pl.semaphore_signal(barrier, 1, device_id=self.in_column(offset), device_id_type=MESH)

    def met(self):
        pl.semaphore_wait(pltpu.get_barrier_semaphore(), len(PLANE) + len(COLUMN))


def remote(src, dst, send, recv, device):
    return pltpu.make_async_remote_copy(
        src_ref=src, dst_ref=dst, send_sem=send, recv_sem=recv, device_id=device, device_id_type=MESH
    )


def started(copies):
    for copy in copies:
        copy.start()
    return copies


def to_tile(value):
    value = value.reshape(-1, 8, value.shape[-1]).sum(0)
    return sum(value[:, k * 128 : (k + 1) * 128] for k in range(value.shape[1] // 128))


def plane_sends(place, tile, slots, sems):
    return started(
        [
            remote(tile, slots.at[place.chip], sems.at[0, i], sems.at[1, i], place.plane(offset))
            for i, offset in enumerate(PLANE)
        ]
    )


def column_sends(place, tile, slots, sems):
    return started(
        [
            remote(tile, slots.at[place.column], sems.at[0, i], sems.at[1, i], place.in_column(offset))
            for i, offset in enumerate(COLUMN)
        ]
    )


def gathered(copies, tile, slots, own):
    slots[own] = tile[...]
    for copy in copies:
        copy.wait()
    return functools.reduce(jnp.add, [slots[k] for k in range(slots.shape[0])])


def gather_kernel(
    grads, accum, whole, clip_out, accum_new, graft_out,
    own, accum_in, tile1, slots1, tile2, slots2,
    load_sem, bulk_sem, pass_sem, plane_sem, column_sem,
):
    place = Place()
    load_grads = pltpu.make_async_copy(grads, own, load_sem.at[0])
    load_accum = pltpu.make_async_copy(accum, accum_in, load_sem.at[1])
    load_grads.start()
    load_accum.start()
    place.greet()
    load_grads.wait()
    squares = jnp.zeros((8, B), F32)
    for block in range(CHIPS):
        wide = own[block].astype(F32)
        squares += (wide * wide).reshape(-1, 8, B).sum(0)
    tile1[...] = to_tile(squares)
    place.met()
    plane = plane_sends(place, tile1, slots1, plane_sem)
    bulk = started(
        [
            remote(
                own.at[place.plane_chip(offset)], whole.at[place.chip, place.c],
                bulk_sem.at[0, i], bulk_sem.at[1, i], place.plane(offset),
            )
            for i, offset in enumerate(PLANE)
        ]
    )
    passed = started(
        [
            remote(
                own.at[place.chip], whole.at[place.chip, place.c],
                pass_sem.at[0, 15], pass_sem.at[1, 15], place.partner,
            )
        ]
    )
    whole[place.chip, place.c] = own[place.chip]
    tile2[...] = gathered(plane, tile1, slots1, place.chip)
    column = column_sends(place, tile2, slots2, column_sem)
    load_accum.wait()
    total = jnp.sum(gathered(column, tile2, slots2, place.column), axis=(0, 1), keepdims=True)
    clip = jnp.minimum(1.0, jnp.sqrt(ENTRIES / (total + 1e-06)))
    clip_out[...] = jnp.broadcast_to(clip, (8, 128))
    graft = jnp.zeros((8, B), F32)
    for i in range(CHIPS):
        if i < 15:
            bulk[14 - i].wait_recv()
            source = place.plane_source(PLANE[14 - i])
            passed += started(
                [
                    remote(
                        whole.at[source, place.c], whole.at[source, place.c],
                        pass_sem.at[0, i], pass_sem.at[1, i], place.partner,
                    )
                ]
            )
        scaled = clip * own[i].astype(F32)
        square = scaled * scaled
        accumulated = accum_in[i] + square
        accum_new[i] = accumulated
        graft += (square / accumulated).reshape(-1, 8, B).sum(0)
    graft_out[...] = to_tile(graft)
    for copy in bulk:
        copy.wait_send()
    for copy in passed:
        copy.wait()


def gather(grads, accum):
    return pl.pallas_call(
        gather_kernel,
        name="gather",
        out_shape=(
            jax.ShapeDtypeStruct((CHIPS, 2, ROWS, B), BF16),
            jax.ShapeDtypeStruct((8, 128), F32),
            jax.ShapeDtypeStruct((CHIPS, ROWS, B), F32),
            jax.ShapeDtypeStruct((8, 128), F32),
        ),
        in_specs=[ANY, ANY],
        out_specs=(VMEM, VMEM, VMEM, VMEM),
        scratch_shapes=[
            pltpu.VMEM((CHIPS, ROWS, B), BF16),
            pltpu.VMEM((CHIPS, ROWS, B), F32),
            pltpu.VMEM((8, 128), F32),
            pltpu.VMEM((CHIPS, 8, 128), F32),
            pltpu.VMEM((8, 128), F32),
            pltpu.VMEM((8, 8, 128), F32),
            pltpu.SemaphoreType.DMA((2,)),
            pltpu.SemaphoreType.DMA((2, 15)),
            pltpu.SemaphoreType.DMA((2, 16)),
            pltpu.SemaphoreType.DMA((2, 15)),
            pltpu.SemaphoreType.DMA((2, 7)),
        ],
        compiler_params=pltpu.CompilerParams(collective_id=0, has_side_effects=True),
    )(grads, accum)


def dot(left, right, contract_left, contract_right):
    return lax.dot_general(
        left, right, (((contract_left,), (contract_right,)), ((), ())), preferred_element_type=F32
    )


def panels():
    for j in range(NT):
        yield slice(j * TILE, (j + 1) * TILE), slice(j * TILE, B), slice((j + 1) * TILE, B)


def symmetric_product(left, right, store):
    for rows, upper, lower in panels():
        value = dot(left[rows, :], right[:, upper], 1, 0)
        store(rows, upper, lower, value)


def mirrored_store(out):
    def store(rows, upper, lower, value):
        value = value.astype(BF16)
        out[rows, upper] = value
        if lower.start < B:
            out[lower, rows] = value[:, TILE:].T

    return store


def plus_diagonal(value, scale):
    row = lax.broadcasted_iota(jnp.int32, value.shape, 0)
    col = lax.broadcasted_iota(jnp.int32, value.shape, 1)
    return jnp.where(row == col, 1.25, 0.0) - scale * value


def factor_store(factor_out, matrix_out):
    def store(rows, upper, lower, value):
        factor = plus_diagonal(value, 0.25).astype(BF16)
        factor_out[rows, upper] = factor
        if lower.start < B:
            factor_out[lower, rows] = factor[:, TILE:].T
        if matrix_out is not None:
            matrix = value.astype(BF16)
            matrix_out[rows, upper] = matrix
            if lower.start < B:
                matrix_out[lower, rows] = matrix[:, TILE:].T

    return store


def roots_kernel(
    whole, clip_in, statistic, accum_in, statistic_new, root, accum_new,
    new, old, factor, matrix, root_a, root_b, square, fourth, sems,
):
    core = lax.axis_index("c")
    load = pltpu.make_async_copy(statistic, old, sems.at[0])
    load.start()
    put_accum = pltpu.make_async_copy(accum_in, accum_new, sems.at[1])
    put_accum.start()

    @pl.when(core == 0)
    def _():
        for rows, upper, _ in panels():
            new[rows, upper] = dot(whole[rows, :], whole[upper, :], 1, 1)

    @pl.when(core == 1)
    def _():
        for rows, upper, _ in panels():
            new[rows, upper] = dot(whole[:, rows], whole[:, upper], 0, 0)

    clip = clip_in[0:1, 0:1]
    weight = 0.1 / B * clip * clip
    load.wait()
    frob = jnp.zeros((8, 128), F32)
    for rows, upper, lower in panels():
        gram = new[rows, upper] * weight
        value = 0.9 * old[rows, upper] + gram
        new[rows, upper] = value
        frob += to_tile(value * value)
        if lower.start < B:
            value = 0.9 * old[lower, rows] + gram[:, TILE:].T
            new[lower, rows] = value
            frob += to_tile(value * value)
    put_new = pltpu.make_async_copy(new, statistic_new, sems.at[2])
    put_new.start()
    total = jnp.sum(to_tile(frob), axis=(0, 1), keepdims=True)
    scale = 2.5 / jnp.sqrt(total + 1e-06)
    start = jnp.sqrt(jnp.sqrt(scale)).astype(BF16).astype(F32)

    @pl.loop(0, B // ROWS)
    def _(i):
        rows = pl.ds(pl.multiple_of(i * ROWS, ROWS), ROWS)
        value = scale * new[rows, :]
        matrix[rows, :] = value.astype(BF16)
        row = lax.broadcasted_iota(jnp.int32, value.shape, 0) + i * ROWS
        col = lax.broadcasted_iota(jnp.int32, value.shape, 1)
        step = (jnp.where(row == col, 1.25, 0.0) - 0.25 * value).astype(BF16)
        factor[rows, :] = step
        root_a[rows, :] = (start * step.astype(F32)).astype(BF16)

    symmetric_product(factor, factor, mirrored_store(square))
    symmetric_product(square, square, mirrored_store(fourth))
    symmetric_product(fourth, matrix, factor_store(factor, square))
    symmetric_product(root_a, factor, mirrored_store(root_b))
    symmetric_product(factor, factor, mirrored_store(matrix))
    symmetric_product(matrix, matrix, mirrored_store(fourth))
    symmetric_product(fourth, square, factor_store(factor, None))
    symmetric_product(root_b, factor, mirrored_store(root))
    put_accum.wait()
    put_new.wait()


def roots(whole, clip, statistic, accum):
    return pl.pallas_call(
        roots_kernel,
        name="roots",
        out_shape=(
            jax.ShapeDtypeStruct((B, B), F32),
            jax.ShapeDtypeStruct((B, B), BF16),
            jax.ShapeDtypeStruct((CHIPS, ROWS, B), F32),
        ),
        in_specs=[VMEM, VMEM, ANY, VMEM],
        out_specs=(ANY, VMEM, ANY),
        scratch_shapes=[pltpu.VMEM((B, B), F32)] * 2
        + [pltpu.VMEM((B, B), BF16)] * 6
        + [pltpu.SemaphoreType.DMA((3,))],
        compiler_params=pltpu.CompilerParams(),
    )(whole, clip, statistic, accum)


RETURN = [PLANE[:8], PLANE[8:] + [(0, 0)]]


def apply_kernel(
    root, whole, graft, back, ratio_out,
    left_rows, right, applied, product, tile1, slots1, tile2, slots2,
    swap_sem, bulk_sem, plane_sem, column_sem,
):
    place = Place()
    place.greet()
    place.met()

    def apply_rows(rows_of, right_root):
        grads = whole[...].reshape(B, B)
        for offsets in RETURN:
            rows = jnp.concatenate([rows_of(place.plane_chip(o)) for o in offsets], axis=0)
            value = dot(rows, grads, 1, 0).astype(BF16)
            for k, o in enumerate(offsets):
                applied[place.plane_chip(o)] = value[k * ROWS : (k + 1) * ROWS]
        return right_root

    def multiply(right_root):
        squares = jnp.zeros((8, B), F32)
        for step, offsets in enumerate(RETURN):
            rows = jnp.concatenate([applied[place.plane_chip(o)] for o in offsets], axis=0)
            value = dot(rows, right_root[...].reshape(B, B), 1, 0)
            squares += (value * value).reshape(-1, 8, B).sum(0)
            if step == 1:
                tile1[0:8] = to_tile(squares)
                tile1[8:16] = graft[...]
                plane_sends(place, tile1, slots1, plane_sem)
            value = value.astype(BF16)
            for k, o in enumerate(offsets):
                chip = place.plane_chip(o)
                product[chip] = value[k * ROWS : (k + 1) * ROWS]
                if o != (0, 0):
                    i = PLANE.index(o)
                    remote(
                        product.at[chip], back.at[place.chip],
                        bulk_sem.at[0, i], bulk_sem.at[1, i], place.plane(o),
                    ).start()
                else:
                    back[place.chip] = value[k * ROWS : (k + 1) * ROWS]

    send_left = remote(root.at[:, 1], left_rows, swap_sem.at[0, 0], swap_sem.at[1, 0], place.partner)
    send_right = remote(root, right, swap_sem.at[0, 1], swap_sem.at[1, 1], place.partner)

    @pl.when(place.c == 0)
    def _():
        send_left.start()
        apply_rows(lambda chip: root[chip, 0], right)
        send_right.wait_recv()
        multiply(right)
        send_left.wait_send()

    @pl.when(place.c == 1)
    def _():
        send_right.start()
        send_left.wait_recv()
        apply_rows(lambda chip: left_rows[chip], root)
        multiply(root)
        send_right.wait_send()

    plane = [
        remote(tile1, slots1.at[place.chip], plane_sem.at[0, i], plane_sem.at[1, i], place.plane(o))
        for i, o in enumerate(PLANE)
    ]
    tile2[...] = gathered(plane, tile1, slots1, place.chip)
    column = column_sends(place, tile2, slots2, column_sem)
    total = gathered(column, tile2, slots2, place.column)
    update_total = jnp.sum(total[0:8], axis=(0, 1), keepdims=True)
    graft_total = jnp.sum(total[8:16], axis=(0, 1), keepdims=True)
    ratio_out[...] = jnp.broadcast_to(jnp.sqrt(graft_total / (update_total + 1e-06)), (8, 128))
    for i, o in enumerate(PLANE):
        remote(
            product.at[place.plane_chip(o)], back.at[place.chip],
            bulk_sem.at[0, i], bulk_sem.at[1, i], place.plane(o),
        ).wait()


def apply(root, whole, graft):
    return pl.pallas_call(
        apply_kernel,
        name="apply",
        out_shape=(
            jax.ShapeDtypeStruct((CHIPS, ROWS, B), BF16),
            jax.ShapeDtypeStruct((8, 128), F32),
        ),
        in_specs=[VMEM, VMEM, VMEM],
        out_specs=(VMEM, VMEM),
        scratch_shapes=[
            pltpu.VMEM((CHIPS, ROWS, B), BF16),
            pltpu.VMEM((CHIPS, 2, ROWS, B), BF16),
            pltpu.VMEM((CHIPS, ROWS, B), BF16),
            pltpu.VMEM((CHIPS, ROWS, B), BF16),
            pltpu.VMEM((16, 128), F32),
            pltpu.VMEM((CHIPS, 16, 128), F32),
            pltpu.VMEM((16, 128), F32),
            pltpu.VMEM((8, 16, 128), F32),
            pltpu.SemaphoreType.DMA((2, 2)),
            pltpu.SemaphoreType.DMA((2, 15)),
            pltpu.SemaphoreType.DMA((2, 15)),
            pltpu.SemaphoreType.DMA((2, 7)),
        ],
        compiler_params=pltpu.CompilerParams(collective_id=1, has_side_effects=True),
    )(root, whole, graft)


def on_device(gradients, statistics, accumulator):
    grads = gradients.reshape(CHIPS, ROWS, B)
    whole, clip, accum, graft = gather(grads, accumulator.reshape(CHIPS, ROWS, B))
    statistic_new, root, accum_new = roots(
        whole.reshape(B, B), clip, statistics.reshape(B, B), accum
    )
    back, ratio = apply(root.reshape(CHIPS, 2, ROWS, B), whole, graft)
    update = ratio[0, 0] * back.astype(F32)
    return (
        update.reshape(gradients.shape),
        statistic_new.reshape(statistics.shape),
        accum_new.reshape(accumulator.shape),
    )


def solution(mesh):
    finer = Mesh(mesh.devices.reshape(4, 4, 2, mesh.shape["mp"]), ("y", "z", "c", "mp"))
    dp = ("y", "z", "c")
    specs = (P(None, "mp", dp, None), P("mp", dp, None, None), P(None, "mp", dp, None))
    return jax.shard_map(on_device, mesh=finer, in_specs=specs, out_specs=specs, check_vma=False)
```

time: 192 us -> 84.5 us (0.44)
  blocking collectives: 94.9 us -> 0 us
  Pallas kernels: 0 us -> 78.9 us
  matrix products: 65.2 us -> 0 us
  starting transfers between devices: 8.4 us -> 0 us
  other arithmetic: 8.96 us -> 3.46 us
  waiting for transfers between devices: 4.13 us -> 0 us
  local copies, waits for them, and re-layouts: 5.35 us -> 1.25 us
  between operations: 3.49 us -> 0.65 us
    pallas_call x0 -> x3, Pallas kernels: none -> 78.9 us  [the longest x1 32.3 us: apply(): pl.pallas_call(apply_kernel, name='apply', out_shape=(jax.ShapeDtypeStruc...]
    psum x8 -> x0, blocking collectives: 65.5 us -> none  [one_axis_at_a_time(): return functools.reduce(lax.psum, axes, value)]
    dot_general x8 -> x0, matrix products: 65.2 us -> none  [the longest x6 50.9 us: batch_dot(): jnp.einsum('kij,kjl->kil', left, right, preferred_element_type=jnp.float32)]
    all_to_all x2 -> x0, blocking collectives: 29.4 us -> none  [moved_by_axis(): result = lax.all_to_all(result, axes[k], k, k, tiled=True)]
    reduce_sum x2 -> x0, other arithmetic: 5.21 us -> none  [the longest x1 4.07 us: on_device(): graft_squares = jnp.sum(graft_step * graft_step)]
    ppermute x2 -> x0, starting transfers between devices: 4.44 us -> none  [partner_2(): lax.ppermute(value, axis, [(i, i ^ 1 << distance) for i in range(lax.axis...]
    ppermute x2 -> x0, waiting for transfers between devices: 4.13 us -> none  [partner_2(): lax.ppermute(value, axis, [(i, i ^ 1 << distance) for i in range(lax.axis...]
    all_to_all x1 -> x0, starting transfers between devices: 3.96 us -> none  [on_device(): lax.all_to_all(pieces.astype(jnp.bfloat16), DP, split_axis=1, concat_axis...]
  transfers between devices with their start and end apart: 3 -> 0, of which waited for: 1 -> 0; matrix products, arithmetic and copies ran while one was open for 3% -> 0% of each run, Pallas kernels for 0% -> 0%
where the time goes in v1:
time: 84.5 us; the launch traced here: 84.3 us
  Pallas kernels  78.9 us (93%)
  other arithmetic  3.46 us (4%)
  local copies, waits for them, and re-layouts  1.25 us (1%)
    pallas_call x1, Pallas kernels, apply(): pl.pallas_call(apply_kernel, name='apply', out_shape=(jax.ShapeDtypeStruc...  32.3 us
    pallas_call x1, Pallas kernels, gather(): pl.pallas_call(gather_kernel, name='gather', out_shape=(jax.ShapeDtypeStr...  26.5 us
    pallas_call x1, Pallas kernels, roots(): pl.pallas_call(roots_kernel, name='roots', out_shape=(jax.ShapeDtypeStruc...  20.1 us
    mul x1, other arithmetic, on_device(): update = ratio[0, 0] * back.astype(F32)  3.46 us

profile of v1, /device:TPU:1, one launch (start us, length us, event | category | flops | bytes accessed | tf_op | source)
XLA Modules:
  0.0 84.3 jit_solution(14959957623827875072)
XLA Ops:
  0.6 26.5 %gather.1 = (bf16[16,2,32,1024]{3,2,1,0:T(8,128)(2,1)}, f32[8,128]{1,0:T(8,128)}, f32[16,32,1024]{2,1,0:T(8,128)}, f32[8,128]{1,0:T(8,128)}) custom-call(bf16[16,32,1024]{2,1,0:T(8,128)(2,1)} %bitcast.14, f32[16,32,1024]{2,1,0:T(8,128)} %bitcast.12), custom_call_target="tpu_custom_call" | custom-call | tf_op jit(solution)/shard_map/gather/pallas_call | solution.py:177
  27.2 20.1 %roots.1 = (f32[1024,1024]{1,0:T(8,128)}, bf16[1024,1024]{1,0:T(8,128)(2,1)}, f32[16,32,1024]{2,1,0:T(8,128)}) custom-call(bf16[1024,1024]{1,0:T(8,128)(2,1)} %bitcast.9, f32[8,128]{1,0:T(8,128)} %get-tuple-element.13.clip_in, f32[1024,1024]{1,0:T(8,128)} %bitcast.10, f32[16,32,1024]{2,1,0:T(8,128)} %get-tuple-element.14.accum_in), custom_call_target="tpu_custom_call" | custom-call | tf_op jit(solution)/shard_map/roots/pallas_call | solution.py:316
  47.3 32.3 %apply.1 = (bf16[16,32,1024]{2,1,0:T(8,128)(2,1)}, f32[8,128]{1,0:T(8,128)}) custom-call(bf16[16,2,32,1024]{3,2,1,0:T(8,128)(2,1)} %bitcast.11, bf16[16,2,32,1024]{3,2,1,0:T(8,128)(2,1)} %get-tuple-element.12.whole, f32[8,128]{1,0:T(8,128)} %get-tuple-element.16.graft), custom_call_target="tpu_custom_call" | custom-call | tf_op jit(solution)/shard_map/apply/pallas_call | solution.py:414
  79.6 1.3 %slice.3 = f32[1,1]{1,0:T(1,128)} slice(f32[8,128]{1,0:T(8,128)} %get-tuple-element.17), slice={[0:1], [0:1]} | slice | bytes 8 | tf_op jit(solution)/shard_map/slice | solution.py:448
  80.8 3.5 %convert_multiply_fusion = f32[16,32,1024]{2,1,0:T(8,128)} fusion(bf16[16,32,1024]{2,1,0:T(8,128)(2,1)} %get-tuple-element.18, f32[]{:T(128)} %bitcast.5), kind=kLoop, calls=%fused_computation | loop fusion | flops 1048576 | bytes 3145732 | tf_op jit(solution)/shard_map/mul | solution.py:448

commit v2 on v1

--- a/solution.py
+++ b/solution.py
@@ -12,7 +12,7 @@
 BF16 = jnp.bfloat16
 MESH = pl.DeviceIdType.MESH
 VMEM = pl.BlockSpec(memory_space=pltpu.VMEM)
-ANY = pl.BlockSpec(memory_space=pl.ANY)
+HBM = pl.BlockSpec(memory_space=pltpu.MemorySpace.HBM)
 
 B = 1024
 TILE = 256
@@ -106,7 +106,7 @@
 
 
 def gather_kernel(
-    grads, accum, whole, clip_out, accum_new, graft_out,
+    grads, accum, statistic, whole, clip_out, accum_new, graft_out, statistic_out,
     own, accum_in, tile1, slots1, tile2, slots2,
     load_sem, bulk_sem, pass_sem, plane_sem, column_sem,
 ):
@@ -114,7 +114,9 @@
     load_grads = pltpu.make_async_copy(grads, own, load_sem.at[0])
     load_accum = pltpu.make_async_copy(accum, accum_in, load_sem.at[1])
     load_grads.start()
+    load_statistic = pltpu.make_async_copy(statistic, statistic_out, load_sem.at[2])
     load_accum.start()
+    load_statistic.start()
     place.greet()
     load_grads.wait()
     squares = jnp.zeros((8, B), F32)
@@ -167,13 +169,14 @@
         accum_new[i] = accumulated
         graft += (square / accumulated).reshape(-1, 8, B).sum(0)
     graft_out[...] = to_tile(graft)
+    load_statistic.wait()
     for copy in bulk:
         copy.wait_send()
     for copy in passed:
         copy.wait()
 
 
-def gather(grads, accum):
+def gather(grads, accum, statistic):
     return pl.pallas_call(
         gather_kernel,
         name="gather",
@@ -182,9 +185,10 @@
             jax.ShapeDtypeStruct((8, 128), F32),
             jax.ShapeDtypeStruct((CHIPS, ROWS, B), F32),
             jax.ShapeDtypeStruct((8, 128), F32),
+            jax.ShapeDtypeStruct((B, B), F32),
         ),
-        in_specs=[ANY, ANY],
-        out_specs=(VMEM, VMEM, VMEM, VMEM),
+        in_specs=[HBM, HBM, HBM],
+        out_specs=(VMEM, VMEM, VMEM, VMEM, VMEM),
         scratch_shapes=[
             pltpu.VMEM((CHIPS, ROWS, B), BF16),
             pltpu.VMEM((CHIPS, ROWS, B), F32),
@@ -192,14 +196,14 @@
             pltpu.VMEM((CHIPS, 8, 128), F32),
             pltpu.VMEM((8, 128), F32),
             pltpu.VMEM((8, 8, 128), F32),
-            pltpu.SemaphoreType.DMA((2,)),
+            pltpu.SemaphoreType.DMA((3,)),
             pltpu.SemaphoreType.DMA((2, 15)),
             pltpu.SemaphoreType.DMA((2, 16)),
             pltpu.SemaphoreType.DMA((2, 15)),
             pltpu.SemaphoreType.DMA((2, 7)),
         ],
-        compiler_params=pltpu.CompilerParams(collective_id=0, has_side_effects=True),
-    )(grads, accum)
+        compiler_params=pltpu.CompilerParams(collective_id=0, has_side_effects=True, vmem_limit_bytes=24 << 20),
+    )(grads, accum, statistic)
 
 
 def dot(left, right, contract_left, contract_right):
@@ -251,13 +255,11 @@
 
 
 def roots_kernel(
-    whole, clip_in, statistic, accum_in, statistic_new, root, accum_new,
-    new, old, factor, matrix, root_a, root_b, square, fourth, sems,
+    whole, clip_in, old, accum_in, statistic_new, root, factor, accum_new,
+    new, matrix, root_a, square, fourth, sems,
 ):
     core = lax.axis_index("c")
-    load = pltpu.make_async_copy(statistic, old, sems.at[0])
-    load.start()
-    put_accum = pltpu.make_async_copy(accum_in, accum_new, sems.at[1])
+    put_accum = pltpu.make_async_copy(accum_in, accum_new, sems.at[0])
     put_accum.start()
 
     @pl.when(core == 0)
@@ -272,7 +274,6 @@
 
     clip = clip_in[0:1, 0:1]
     weight = 0.1 / B * clip * clip
-    load.wait()
     frob = jnp.zeros((8, 128), F32)
     for rows, upper, lower in panels():
         gram = new[rows, upper] * weight
@@ -283,9 +284,9 @@
             value = 0.9 * old[lower, rows] + gram[:, TILE:].T
             new[lower, rows] = value
             frob += to_tile(value * value)
-    put_new = pltpu.make_async_copy(new, statistic_new, sems.at[2])
+    put_new = pltpu.make_async_copy(new, statistic_new, sems.at[1])
     put_new.start()
-    total = jnp.sum(to_tile(frob), axis=(0, 1), keepdims=True)
+    total = jnp.sum(frob, axis=(0, 1), keepdims=True)
     scale = 2.5 / jnp.sqrt(total + 1e-06)
     start = jnp.sqrt(jnp.sqrt(scale)).astype(BF16).astype(F32)
 
@@ -303,11 +304,10 @@
     symmetric_product(factor, factor, mirrored_store(square))
     symmetric_product(square, square, mirrored_store(fourth))
     symmetric_product(fourth, matrix, factor_store(factor, square))
-    symmetric_product(root_a, factor, mirrored_store(root_b))
+    symmetric_product(root_a, factor, mirrored_store(root))
     symmetric_product(factor, factor, mirrored_store(matrix))
     symmetric_product(matrix, matrix, mirrored_store(fourth))
     symmetric_product(fourth, square, factor_store(factor, None))
-    symmetric_product(root_b, factor, mirrored_store(root))
     put_accum.wait()
     put_new.wait()
 
@@ -319,133 +319,178 @@
         out_shape=(
             jax.ShapeDtypeStruct((B, B), F32),
             jax.ShapeDtypeStruct((B, B), BF16),
+            jax.ShapeDtypeStruct((B, B), BF16),
             jax.ShapeDtypeStruct((CHIPS, ROWS, B), F32),
         ),
-        in_specs=[VMEM, VMEM, ANY, VMEM],
-        out_specs=(ANY, VMEM, ANY),
-        scratch_shapes=[pltpu.VMEM((B, B), F32)] * 2
-        + [pltpu.VMEM((B, B), BF16)] * 6
-        + [pltpu.SemaphoreType.DMA((3,))],
-        compiler_params=pltpu.CompilerParams(),
+        in_specs=[VMEM, VMEM, VMEM, VMEM],
+        out_specs=(HBM, VMEM, VMEM, HBM),
+        scratch_shapes=[pltpu.VMEM((B, B), F32)]
+        + [pltpu.VMEM((B, B), BF16)] * 4
+        + [pltpu.SemaphoreType.DMA((2,))],
+        compiler_params=pltpu.CompilerParams(vmem_limit_bytes=32 << 20),
     )(whole, clip, statistic, accum)
 
 
-RETURN = [PLANE[:8], PLANE[8:] + [(0, 0)]]
-
-
 def apply_kernel(
-    root, whole, graft, back, ratio_out,
-    left_rows, right, applied, product, tile1, slots1, tile2, slots2,
-    swap_sem, bulk_sem, plane_sem, column_sem,
+    root, factor, whole, graft, back, ratio_out,
+    both, applied, product, tile1, slots1, tile2, slots2,
+    left_sem, right_sem, bulk_sem, plane_sem, column_sem,
 ):
     place = Place()
     place.greet()
-    place.met()
-
-    def apply_rows(rows_of, right_root):
-        grads = whole[...].reshape(B, B)
-        for offsets in RETURN:
-            rows = jnp.concatenate([rows_of(place.plane_chip(o)) for o in offsets], axis=0)
-            value = dot(rows, grads, 1, 0).astype(BF16)
-            for k, o in enumerate(offsets):
-                applied[place.plane_chip(o)] = value[k * ROWS : (k + 1) * ROWS]
-        return right_root
-
-    def multiply(right_root):
-        squares = jnp.zeros((8, B), F32)
-        for step, offsets in enumerate(RETURN):
-            rows = jnp.concatenate([applied[place.plane_chip(o)] for o in offsets], axis=0)
-            value = dot(rows, right_root[...].reshape(B, B), 1, 0)
-            squares += (value * value).reshape(-1, 8, B).sum(0)
-            if step == 1:
-                tile1[0:8] = to_tile(squares)
-                tile1[8:16] = graft[...]
-                plane_sends(place, tile1, slots1, plane_sem)
-            value = value.astype(BF16)
-            for k, o in enumerate(offsets):
-                chip = place.plane_chip(o)
-                product[chip] = value[k * ROWS : (k + 1) * ROWS]
-                if o != (0, 0):
-                    i = PLANE.index(o)
-                    remote(
-                        product.at[chip], back.at[place.chip],
-                        bulk_sem.at[0, i], bulk_sem.at[1, i], place.plane(o),
-                    ).start()
-                else:
-                    back[place.chip] = value[k * ROWS : (k + 1) * ROWS]
-
-    send_left = remote(root.at[:, 1], left_rows, swap_sem.at[0, 0], swap_sem.at[1, 0], place.partner)
-    send_right = remote(root, right, swap_sem.at[0, 1], swap_sem.at[1, 1], place.partner)
-
-    @pl.when(place.c == 0)
-    def _():
-        send_left.start()
-        apply_rows(lambda chip: root[chip, 0], right)
-        send_right.wait_recv()
-        multiply(right)
-        send_left.wait_send()
+
+    def swap_left(j):
+        chips = pl.ds(4 * j, 4)
+        return remote(
+            both.at[0, chips, 1], both.at[0, chips, 1],
+            left_sem.at[0, j], left_sem.at[1, j], place.partner,
+        )
+
+    def swap_right(j):
+        part = (1, pl.ds(4 * j, 4), slice(None), slice(None), pl.ds(j * TILE, B - j * TILE))
+        return remote(
+            both.at[part], both.at[part], right_sem.at[0, j], right_sem.at[1, j], place.partner
+        )
+
+    def give_back(j, i):
+        return remote(
+            product.at[j, place.plane_chip(PLANE[i])], back.at[j, place.chip],
+            bulk_sem.at[0, j, i], bulk_sem.at[1, j, i], place.plane(PLANE[i]),
+        )
+
+    for j, (rows, upper, lower) in enumerate(panels()):
+        value = dot(root[rows, :], factor[:, upper], 1, 0).astype(BF16)
+        both[place.c, 4 * j : 4 * j + 4, :, :, upper] = value.reshape(4, 2, ROWS, -1)
+        if lower.start < B:
+            mirror = value[:, TILE:].T
+            both[place.c, 4 * j + 4 : CHIPS, :, :, rows] = mirror.reshape(-1, 2, ROWS, TILE)
+        if j == 0:
+            place.met()
+
+        @pl.when(place.c == 0)
+        def _(j=j):
+            swap_left(j).start()
+
+        @pl.when(place.c == 1)
+        def _(j=j):
+            swap_right(j).start()
 
     @pl.when(place.c == 1)
     def _():
-        send_right.start()
-        send_left.wait_recv()
-        apply_rows(lambda chip: left_rows[chip], root)
-        multiply(root)
-        send_right.wait_send()
-
-    plane = [
-        remote(tile1, slots1.at[place.chip], plane_sem.at[0, i], plane_sem.at[1, i], place.plane(o))
-        for i, o in enumerate(PLANE)
-    ]
+        for j in range(NT):
+            swap_left(j).wait_recv()
+
+    left_rows = both[0, :, place.c].reshape(B // 2, B)
+    applied[...] = dot(left_rows, whole[...], 1, 0).astype(BF16)
+    squares = jnp.zeros((8, 128), F32)
+    for j, (rows, upper, _) in enumerate(panels()):
+
+        @pl.when(place.c == 0)
+        def _(j=j):
+            swap_right(j).wait_recv()
+
+        right_rows = both[1, 4 * j : 4 * j + 4, :, :, upper].reshape(TILE, -1)
+        value = dot(applied[:, upper], right_rows, 1, 1)
+        if j:
+            value += dot(applied[:, : j * TILE], both[1, : 4 * j, :, :, rows].reshape(-1, TILE), 1, 0)
+        squares += to_tile(value * value)
+        product[j] = value.astype(BF16).reshape(CHIPS, ROWS, TILE)
+        if j == NT - 1:
+            tile1[0:8] = squares
+            tile1[8:16] = graft[...]
+            plane = plane_sends(place, tile1, slots1, plane_sem)
+        for i in range(len(PLANE)):
+            give_back(j, i).start()
+        back[j, place.chip] = product[j, place.chip]
+
     tile2[...] = gathered(plane, tile1, slots1, place.chip)
     column = column_sends(place, tile2, slots2, column_sem)
     total = gathered(column, tile2, slots2, place.column)
     update_total = jnp.sum(total[0:8], axis=(0, 1), keepdims=True)
     graft_total = jnp.sum(total[8:16], axis=(0, 1), keepdims=True)
     ratio_out[...] = jnp.broadcast_to(jnp.sqrt(graft_total / (update_total + 1e-06)), (8, 128))
-    for i, o in enumerate(PLANE):
-        remote(
-            product.at[place.plane_chip(o)], back.at[place.chip],
-            bulk_sem.at[0, i], bulk_sem.at[1, i], place.plane(o),
-        ).wait()
-
-
-def apply(root, whole, graft):
+
+    @pl.when(place.c == 0)
+    def _():
+        for j in range(NT):
+            swap_left(j).wait_send()
+
+    @pl.when(place.c == 1)
+    def _():
+        for j in range(NT):
+            swap_right(j).wait_send()
+
+    for j in range(NT):
+        for i in range(len(PLANE)):
+            give_back(j, i).wait()
+
+
+def apply(root, factor, whole, graft):
     return pl.pallas_call(
         apply_kernel,
         name="apply",
         out_shape=(
-            jax.ShapeDtypeStruct((CHIPS, ROWS, B), BF16),
+            jax.ShapeDtypeStruct((NT, CHIPS, ROWS, TILE), BF16),
             jax.ShapeDtypeStruct((8, 128), F32),
         ),
-        in_specs=[VMEM, VMEM, VMEM],
+        in_specs=[VMEM, VMEM, VMEM, VMEM],
         out_specs=(VMEM, VMEM),
         scratch_shapes=[
-            pltpu.VMEM((CHIPS, ROWS, B), BF16),
-            pltpu.VMEM((CHIPS, 2, ROWS, B), BF16),
-            pltpu.VMEM((CHIPS, ROWS, B), BF16),
-            pltpu.VMEM((CHIPS, ROWS, B), BF16),
+            pltpu.VMEM((2, CHIPS, 2, ROWS, B), BF16),
+            pltpu.VMEM((B // 2, B), BF16),
+            pltpu.VMEM((NT, CHIPS, ROWS, TILE), BF16),
             pltpu.VMEM((16, 128), F32),
             pltpu.VMEM((CHIPS, 16, 128), F32),
             pltpu.VMEM((16, 128), F32),
             pltpu.VMEM((8, 16, 128), F32),
-            pltpu.SemaphoreType.DMA((2, 2)),
-            pltpu.SemaphoreType.DMA((2, 15)),
+            pltpu.SemaphoreType.DMA((2, NT)),
+            pltpu.SemaphoreType.DMA((2, NT)),
+            pltpu.SemaphoreType.DMA((2, NT, 15)),
             pltpu.SemaphoreType.DMA((2, 15)),
             pltpu.SemaphoreType.DMA((2, 7)),
         ],
-        compiler_params=pltpu.CompilerParams(collective_id=1, has_side_effects=True),
-    )(root, whole, graft)
+        compiler_params=pltpu.CompilerParams(
+            collective_id=1, has_side_effects=True, vmem_limit_bytes=24 << 20
+        ),
+    )(root, factor, whole, graft)
+
+
+def scale_kernel(back, ratio, update, wide, sems):
+    factor = ratio[0:1, 0:1]
+    puts = []
+    for group in range(4):
+        for chip in range(4 * group, 4 * group + 4):
+            for j in range(NT):
+                wide[chip, :, j * TILE : (j + 1) * TILE] = factor * back[j, chip].astype(F32)
+        chips = pl.ds(4 * group, 4)
+        puts += started([pltpu.make_async_copy(wide.at[chips], update.at[chips], sems.at[group])])
+    for put in puts:
+        put.wait()
+
+
+def scale(back, ratio):
+    return pl.pallas_call(
+        scale_kernel,
+        name="scale",
+        out_shape=jax.ShapeDtypeStruct((CHIPS, ROWS, B), F32),
+        in_specs=[VMEM, VMEM],
+        out_specs=HBM,
+        scratch_shapes=[pltpu.VMEM((CHIPS, ROWS, B), F32), pltpu.SemaphoreType.DMA((4,))],
+        compiler_params=pltpu.CompilerParams(vmem_limit_bytes=16 << 20),
+    )(back, ratio)
 
 
 def on_device(gradients, statistics, accumulator):
+    in_hbm = functools.partial(
+        pltpu.with_memory_space_constraint, memory_space=pltpu.MemorySpace.HBM
+    )
     grads = gradients.reshape(CHIPS, ROWS, B)
-    whole, clip, accum, graft = gather(grads, accumulator.reshape(CHIPS, ROWS, B))
-    statistic_new, root, accum_new = roots(
-        whole.reshape(B, B), clip, statistics.reshape(B, B), accum
-    )
-    back, ratio = apply(root.reshape(CHIPS, 2, ROWS, B), whole, graft)
-    update = ratio[0, 0] * back.astype(F32)
+    whole, clip, accum, graft, statistic = gather(
+        in_hbm(grads), in_hbm(accumulator.reshape(CHIPS, ROWS, B)), in_hbm(statistics.reshape(B, B))
+    )
+    whole = whole.reshape(B, B)
+    statistic_new, root, factor, accum_new = roots(whole, clip, statistic, accum)
+    update = scale(*apply(root, factor, whole, graft))
     return (
         update.reshape(gradients.shape),
         statistic_new.reshape(statistics.shape),

time: 84.5 us -> 70.2 us (0.83)
  Pallas kernels: 78.9 us -> 69.2 us
  other arithmetic: 3.46 us -> 0 us
  local copies, waits for them, and re-layouts: 1.25 us -> 0 us
    pallas_call x1, Pallas kernels: 20.1 us -> 14.1 us  [roots(): pl.pallas_call(roots_kernel, name='roots', out_shape=(jax.ShapeDtypeStruc...]
    mul x1 -> x0, other arithmetic: 3.46 us -> none  [on_device(): update = ratio[0, 0] * back.astype(F32)]
    pallas_call x1, Pallas kernels: 32.3 us -> 29.1 us  [apply(): pl.pallas_call(apply_kernel, name='apply', out_shape=(jax.ShapeDtypeStruc...]
    pallas_call x1, Pallas kernels: 26.5 us -> 24.6 us  [gather(): pl.pallas_call(gather_kernel, name='gather', out_shape=(jax.ShapeDtypeStr...]
    pallas_call x0 -> x1, Pallas kernels: none -> 1.42 us  [scale(): pl.pallas_call(scale_kernel, name='scale', out_shape=jax.ShapeDtypeStruct...]
    slice x1 -> x0, local copies, waits for them, and re-layouts: 1.25 us -> none  [on_device(): update = ratio[0, 0] * back.astype(F32)]
where the time goes in v2:
time: 70.2 us; the launch traced here: 70.1 us
  Pallas kernels  69.2 us (99%)
  between operations  0.81 us (1%)
    pallas_call x1, Pallas kernels, apply(): pl.pallas_call(apply_kernel, name='apply', out_shape=(jax.ShapeDtypeStruc...  29.1 us
    pallas_call x1, Pallas kernels, gather(): pl.pallas_call(gather_kernel, name='gather', out_shape=(jax.ShapeDtypeStr...  24.6 us
    pallas_call x1, Pallas kernels, roots(): pl.pallas_call(roots_kernel, name='roots', out_shape=(jax.ShapeDtypeStruc...  14.1 us
    pallas_call x1, Pallas kernels, scale(): pl.pallas_call(scale_kernel, name='scale', out_shape=jax.ShapeDtypeStruct...  1.42 us

profile of v2, /device:TPU:1, one launch (start us, length us, event | category | flops | bytes accessed | tf_op | source)
XLA Modules:
  0.0 70.1 jit_solution(11710339067503563513)
XLA Ops:
  0.6 24.6 %gather.1 = (bf16[16,2,32,1024]{3,2,1,0:T(8,128)(2,1)S(1)}, f32[8,128]{1,0:T(8,128)S(1)}, f32[16,32,1024]{2,1,0:T(8,128)S(1)}, f32[8,128]{1,0:T(8,128)S(1)}, f32[1024,1024]{1,0:T(8,128)S(1)}) custom-call(bf16[16,32,1024]{2,1,0:T(8,128)(2,1)} %bitcast.12, f32[16,32,1024]{2,1,0:T(8,128)} %bitcast.10, f32[1024,1024]{1,0:T(8,128)} %bitcast.9), custom_call_target="tpu_custom_call" | custom-call | tf_op jit(solution)/shard_map/gather/pallas_call | solution.py:180
  25.3 14.1 %roots.1 = (f32[1024,1024]{1,0:T(8,128)}, bf16[1024,1024]{1,0:T(8,128)(2,1)S(1)}, bf16[1024,1024]{1,0:T(8,128)(2,1)S(1)}, f32[16,32,1024]{2,1,0:T(8,128)}) custom-call(bf16[1024,1024]{1,0:T(8,128)(2,1)S(1)} %bitcast.7, f32[8,128]{1,0:T(8,128)S(1)} %get-tuple-element.15.clip_in, f32[1024,1024]{1,0:T(8,128)S(1)} %get-tuple-element.16.old, ...), custom_call_target="tpu_custom_call" | custom-call | tf_op jit(solution)/shard_map/roots/pallas_call | solution.py:316
  39.4 29.1 %apply.1 = (bf16[4,16,32,256]{3,2,1,0:T(8,128)(2,1)S(1)}, f32[8,128]{1,0:T(8,128)S(1)}) custom-call(bf16[1024,1024]{1,0:T(8,128)(2,1)S(1)} %get-tuple-element.18.root, bf16[1024,1024]{1,0:T(8,128)(2,1)S(1)} %get-tuple-element.19.factor, bf16[1024,1024]{1,0:T(8,128)(2,1)S(1)} %bitcast.8, f32[8,128]{1,0:T(8,128)S(1)} %get-tuple-element.20.graft), custom_call_target="tpu_custom_call" | custom-call | tf_op jit(solution)/shard_map/apply/pallas_call | solution.py:429
  68.5 1.4 %scale.1 = f32[16,32,1024]{2,1,0:T(8,128)} custom-call(bf16[4,16,32,256]{3,2,1,0:T(8,128)(2,1)S(1)} %get-tuple-element.21.back, f32[8,128]{1,0:T(8,128)S(1)} %get-tuple-element.22.ratio), custom_call_target="tpu_custom_call" | custom-call | tf_op jit(solution)/shard_map/scale/pallas_call | solution.py:472

commit v3 on v2

--- a/solution.py
+++ b/solution.py
@@ -28,7 +28,7 @@
 
 PLANE = sorted(
     [(dy, dz) for dy in range(4) for dz in range(4) if (dy, dz) != (0, 0)],
-    key=lambda offset: -ring_distance(offset),
+    key=ring_distance,
 )
 COLUMN = [(dx, dc) for dx in range(4) for dc in range(2) if (dx, dc) != (0, 0)]
 
@@ -81,21 +81,17 @@
 
 
 def plane_sends(place, tile, slots, sems):
-    return started(
-        [
-            remote(tile, slots.at[place.chip], sems.at[0, i], sems.at[1, i], place.plane(offset))
-            for i, offset in enumerate(PLANE)
-        ]
-    )
+    return [
+        remote(tile, slots.at[place.chip], sems.at[0, i], sems.at[1, i], place.plane(offset))
+        for i, offset in enumerate(PLANE)
+    ]
 
 
 def column_sends(place, tile, slots, sems):
-    return started(
-        [
-            remote(tile, slots.at[place.column], sems.at[0, i], sems.at[1, i], place.in_column(offset))
-            for i, offset in enumerate(COLUMN)
-        ]
-    )
+    return [
+        remote(tile, slots.at[place.column], sems.at[0, i], sems.at[1, i], place.in_column(offset))
+        for i, offset in enumerate(COLUMN)
+    ]
 
 
 def gathered(copies, tile, slots, own):
@@ -115,8 +111,6 @@
     load_accum = pltpu.make_async_copy(accum, accum_in, load_sem.at[1])
     load_grads.start()
     load_statistic = pltpu.make_async_copy(statistic, statistic_out, load_sem.at[2])
-    load_accum.start()
-    load_statistic.start()
     place.greet()
     load_grads.wait()
     squares = jnp.zeros((8, B), F32)
@@ -124,8 +118,10 @@
         wide = own[block].astype(F32)
         squares += (wide * wide).reshape(-1, 8, B).sum(0)
     tile1[...] = to_tile(squares)
+    load_accum.start()
+    load_statistic.start()
     place.met()
-    plane = plane_sends(place, tile1, slots1, plane_sem)
+    plane = started(plane_sends(place, tile1, slots1, plane_sem))
     bulk = started(
         [
             remote(
@@ -145,7 +141,7 @@
     )
     whole[place.chip, place.c] = own[place.chip]
     tile2[...] = gathered(plane, tile1, slots1, place.chip)
-    column = column_sends(place, tile2, slots2, column_sem)
+    column = started(column_sends(place, tile2, slots2, column_sem))
     load_accum.wait()
     total = jnp.sum(gathered(column, tile2, slots2, place.column), axis=(0, 1), keepdims=True)
     clip = jnp.minimum(1.0, jnp.sqrt(ENTRIES / (total + 1e-06)))
@@ -153,8 +149,8 @@
     graft = jnp.zeros((8, B), F32)
     for i in range(CHIPS):
         if i < 15:
-            bulk[14 - i].wait_recv()
-            source = place.plane_source(PLANE[14 - i])
+            bulk[i].wait_recv()
+            source = place.plane_source(PLANE[i])
             passed += started(
                 [
                     remote(
@@ -255,8 +251,8 @@
 
 
 def roots_kernel(
-    whole, clip_in, old, accum_in, statistic_new, root, factor, accum_new,
-    new, matrix, root_a, square, fourth, sems,
+    whole, clip_in, old, accum_in, statistic_new, root_a, factor, matrix_out, accum_new,
+    new, matrix, square, fourth, sems,
 ):
     core = lax.axis_index("c")
     put_accum = pltpu.make_async_copy(accum_in, accum_new, sems.at[0])
@@ -303,11 +299,7 @@
 
     symmetric_product(factor, factor, mirrored_store(square))
     symmetric_product(square, square, mirrored_store(fourth))
-    symmetric_product(fourth, matrix, factor_store(factor, square))
-    symmetric_product(root_a, factor, mirrored_store(root))
-    symmetric_product(factor, factor, mirrored_store(matrix))
-    symmetric_product(matrix, matrix, mirrored_store(fourth))
-    symmetric_product(fourth, square, factor_store(factor, None))
+    symmetric_product(fourth, matrix, factor_store(factor, matrix_out))
     put_accum.wait()
     put_new.wait()
 
@@ -320,20 +312,21 @@
             jax.ShapeDtypeStruct((B, B), F32),
             jax.ShapeDtypeStruct((B, B), BF16),
             jax.ShapeDtypeStruct((B, B), BF16),
+            jax.ShapeDtypeStruct((B, B), BF16),
             jax.ShapeDtypeStruct((CHIPS, ROWS, B), F32),
         ),
         in_specs=[VMEM, VMEM, VMEM, VMEM],
-        out_specs=(HBM, VMEM, VMEM, HBM),
+        out_specs=(HBM, VMEM, VMEM, VMEM, HBM),
         scratch_shapes=[pltpu.VMEM((B, B), F32)]
-        + [pltpu.VMEM((B, B), BF16)] * 4
+        + [pltpu.VMEM((B, B), BF16)] * 3
         + [pltpu.SemaphoreType.DMA((2,))],
         compiler_params=pltpu.CompilerParams(vmem_limit_bytes=32 << 20),
     )(whole, clip, statistic, accum)
 
 
 def apply_kernel(
-    root, factor, whole, graft, back, ratio_out,
-    both, applied, product, tile1, slots1, tile2, slots2,
+    root_a, factor_a, matrix, whole, graft, back, ratio_out,
+    root, factor, square, fourth, both, applied, product, tile1, slots1, tile2, slots2,
     left_sem, right_sem, bulk_sem, plane_sem, column_sem,
 ):
     place = Place()
@@ -358,36 +351,48 @@
             bulk_sem.at[0, j, i], bulk_sem.at[1, j, i], place.plane(PLANE[i]),
         )
 
+    symmetric_product(root_a, factor_a, mirrored_store(root))
+    symmetric_product(factor_a, factor_a, mirrored_store(square))
+    symmetric_product(square, square, mirrored_store(fourth))
+    symmetric_product(fourth, matrix, factor_store(factor, None))
+    place.met()
     for j, (rows, upper, lower) in enumerate(panels()):
         value = dot(root[rows, :], factor[:, upper], 1, 0).astype(BF16)
         both[place.c, 4 * j : 4 * j + 4, :, :, upper] = value.reshape(4, 2, ROWS, -1)
         if lower.start < B:
             mirror = value[:, TILE:].T
             both[place.c, 4 * j + 4 : CHIPS, :, :, rows] = mirror.reshape(-1, 2, ROWS, TILE)
-        if j == 0:
-            place.met()
-
-        @pl.when(place.c == 0)
-        def _(j=j):
-            swap_left(j).start()
+
+        if j % 2:
+
+            @pl.when(place.c == 0)
+            def _(j=j):
+                swap_left(j - 1).start()
+                swap_left(j).start()
+
+            @pl.when(place.c == 1)
+            def _(j=j):
+                swap_right(j - 1).start()
+                swap_right(j).start()
+
+    for half in range(2):
 
         @pl.when(place.c == 1)
-        def _(j=j):
-            swap_right(j).start()
-
-    @pl.when(place.c == 1)
-    def _():
-        for j in range(NT):
-            swap_left(j).wait_recv()
-
-    left_rows = both[0, :, place.c].reshape(B // 2, B)
-    applied[...] = dot(left_rows, whole[...], 1, 0).astype(BF16)
+        def _(half=half):
+            for j in (2 * half, 2 * half + 1):
+                swap_left(j).wait_recv()
+
+        left_rows = both[0, 8 * half : 8 * half + 8, place.c].reshape(TILE, B)
+        applied[half * TILE : (half + 1) * TILE] = dot(left_rows, whole[...], 1, 0).astype(BF16)
     squares = jnp.zeros((8, 128), F32)
     for j, (rows, upper, _) in enumerate(panels()):
 
-        @pl.when(place.c == 0)
-        def _(j=j):
-            swap_right(j).wait_recv()
+        if j == 0:
+
+            @pl.when(place.c == 0)
+            def _():
+                for i in range(NT):
+                    swap_right(i).wait_recv()
 
         right_rows = both[1, 4 * j : 4 * j + 4, :, :, upper].reshape(TILE, -1)
         value = dot(applied[:, upper], right_rows, 1, 1)
@@ -398,13 +403,14 @@
         if j == NT - 1:
             tile1[0:8] = squares
             tile1[8:16] = graft[...]
-            plane = plane_sends(place, tile1, slots1, plane_sem)
-        for i in range(len(PLANE)):
-            give_back(j, i).start()
+            plane = started(plane_sends(place, tile1, slots1, plane_sem))
+        for panel in {0: [0], NT - 1: range(1, NT)}.get(j, []):
+            for i in range(len(PLANE)):
+                give_back(panel, i).start()
         back[j, place.chip] = product[j, place.chip]
 
     tile2[...] = gathered(plane, tile1, slots1, place.chip)
-    column = column_sends(place, tile2, slots2, column_sem)
+    column = started(column_sends(place, tile2, slots2, column_sem))
     total = gathered(column, tile2, slots2, place.column)
     update_total = jnp.sum(total[0:8], axis=(0, 1), keepdims=True)
     graft_total = jnp.sum(total[8:16], axis=(0, 1), keepdims=True)
@@ -425,7 +431,7 @@
             give_back(j, i).wait()
 
 
-def apply(root, factor, whole, graft):
+def apply(root, factor, matrix, whole, graft):
     return pl.pallas_call(
         apply_kernel,
         name="apply",
@@ -433,9 +439,10 @@
             jax.ShapeDtypeStruct((NT, CHIPS, ROWS, TILE), BF16),
             jax.ShapeDtypeStruct((8, 128), F32),
         ),
-        in_specs=[VMEM, VMEM, VMEM, VMEM],
+        in_specs=[VMEM, VMEM, VMEM, VMEM, VMEM],
         out_specs=(VMEM, VMEM),
-        scratch_shapes=[
+        scratch_shapes=[pltpu.VMEM((B, B), BF16)] * 4
+        + [
             pltpu.VMEM((2, CHIPS, 2, ROWS, B), BF16),
             pltpu.VMEM((B // 2, B), BF16),
             pltpu.VMEM((NT, CHIPS, ROWS, TILE), BF16),
@@ -450,9 +457,9 @@
             pltpu.SemaphoreType.DMA((2, 7)),
         ],
         compiler_params=pltpu.CompilerParams(
-            collective_id=1, has_side_effects=True, vmem_limit_bytes=24 << 20
+            collective_id=1, has_side_effects=True, vmem_limit_bytes=32 << 20
         ),
-    )(root, factor, whole, graft)
+    )(root, factor, matrix, whole, graft)
 
 
 def scale_kernel(back, ratio, update, wide, sems):
@@ -489,8 +496,8 @@
         in_hbm(grads), in_hbm(accumulator.reshape(CHIPS, ROWS, B)), in_hbm(statistics.reshape(B, B))
     )
     whole = whole.reshape(B, B)
-    statistic_new, root, factor, accum_new = roots(whole, clip, statistic, accum)
-    update = scale(*apply(root, factor, whole, graft))
+    statistic_new, root, factor, matrix, accum_new = roots(whole, clip, statistic, accum)
+    update = scale(*apply(root, factor, matrix, whole, graft))
     return (
         update.reshape(gradients.shape),
         statistic_new.reshape(statistics.shape),

time: 70.2 us -> 65.2 us (0.929)
  Pallas kernels: 69.2 us -> 64.3 us
    pallas_call x1, Pallas kernels: 14.1 us -> 8.63 us  [roots(): pl.pallas_call(roots_kernel, name='roots', out_shape=(jax.ShapeDtypeStruc...]
    pallas_call x1, Pallas kernels: 24.6 us -> 25.9 us  [gather(): pl.pallas_call(gather_kernel, name='gather', out_shape=(jax.ShapeDtypeStr...]
    pallas_call x1, Pallas kernels: 29.1 us -> 28.3 us  [apply(): pl.pallas_call(apply_kernel, name='apply', out_shape=(jax.ShapeDtypeStruc...]
where the time goes in v3:
time: 65.2 us; the launch traced here: 65.1 us
  Pallas kernels  64.3 us (99%)
  between operations  0.81 us (1%)
    pallas_call x1, Pallas kernels, apply(): pl.pallas_call(apply_kernel, name='apply', out_shape=(jax.ShapeDtypeStruc...  28.3 us
    pallas_call x1, Pallas kernels, gather(): pl.pallas_call(gather_kernel, name='gather', out_shape=(jax.ShapeDtypeStr...  25.9 us
    pallas_call x1, Pallas kernels, roots(): pl.pallas_call(roots_kernel, name='roots', out_shape=(jax.ShapeDtypeStruc...  8.63 us
    pallas_call x1, Pallas kernels, scale(): pl.pallas_call(scale_kernel, name='scale', out_shape=jax.ShapeDtypeStruct...  1.42 us

profile of v3, /device:TPU:1, one launch (start us, length us, event | category | flops | bytes accessed | tf_op | source)
XLA Modules:
  0.0 65.1 jit_solution(16314808655882268723)
XLA Ops:
  0.6 25.9 %gather.1 = (bf16[16,2,32,1024]{3,2,1,0:T(8,128)(2,1)S(1)}, f32[8,128]{1,0:T(8,128)S(1)}, f32[16,32,1024]{2,1,0:T(8,128)S(1)}, f32[8,128]{1,0:T(8,128)S(1)}, f32[1024,1024]{1,0:T(8,128)S(1)}) custom-call(bf16[16,32,1024]{2,1,0:T(8,128)(2,1)} %bitcast.12, f32[16,32,1024]{2,1,0:T(8,128)} %bitcast.10, f32[1024,1024]{1,0:T(8,128)} %bitcast.9), custom_call_target="tpu_custom_call" | custom-call | tf_op jit(solution)/shard_map/gather/pallas_call | solution.py:176
  26.6 8.6 %roots.1 = (f32[1024,1024]{1,0:T(8,128)}, bf16[1024,1024]{1,0:T(8,128)(2,1)S(1)}, bf16[1024,1024]{1,0:T(8,128)(2,1)S(1)}, bf16[1024,1024]{1,0:T(8,128)(2,1)S(1)}, f32[16,32,1024]{2,1,0:T(8,128)}) custom-call(bf16[1024,1024]{1,0:T(8,128)(2,1)S(1)} %bitcast.7, f32[8,128]{1,0:T(8,128)S(1)} %get-tuple-element.16.clip_in, ...), custom_call_target="tpu_custom_call" | custom-call | tf_op jit(solution)/shard_map/roots/pallas_call | solution.py:308
  35.2 28.3 %apply.1 = (bf16[4,16,32,256]{3,2,1,0:T(8,128)(2,1)S(1)}, f32[8,128]{1,0:T(8,128)S(1)}) custom-call(bf16[1024,1024]{1,0:T(8,128)(2,1)S(1)} %get-tuple-element.19.root_a, bf16[1024,1024]{1,0:T(8,128)(2,1)S(1)} %get-tuple-element.20.factor_a, bf16[1024,1024]{1,0:T(8,128)(2,1)S(1)} %get-tuple-element.21.matrix, bf16[1024,1024]{1,0:T(8,128)(2,1)S(1)} %bitcast.8, ...), custom_call_target="tpu_custom_call" | custom-call | tf_op jit(solution)/shard_map/apply/pallas_call | solution.py:435
  63.5 1.4 %scale.1 = f32[16,32,1024]{2,1,0:T(8,128)} custom-call(bf16[4,16,32,256]{3,2,1,0:T(8,128)(2,1)S(1)} %get-tuple-element.23.back, f32[8,128]{1,0:T(8,128)S(1)} %get-tuple-element.24.ratio), custom_call_target="tpu_custom_call" | custom-call | tf_op jit(solution)/shard_map/scale/pallas_call | solution.py:479

commit v4 on v3

--- a/solution.py
+++ b/solution.py
@@ -28,9 +28,15 @@
 
 PLANE = sorted(
     [(dy, dz) for dy in range(4) for dz in range(4) if (dy, dz) != (0, 0)],
-    key=ring_distance,
+    key=lambda offset: (offset[0] == 2, ring_distance(offset)),
 )
 COLUMN = [(dx, dc) for dx in range(4) for dc in range(2) if (dx, dc) != (0, 0)]
+
+ORDER = (0, 1, 3, 2)
+POSITION = [ORDER.index(step) for step in range(4)]
+SEND = sorted(range(len(PLANE)), key=lambda i: ring_distance(PLANE[i]))
+RETURN = sorted(range(len(PLANE)), key=lambda i: -ring_distance(PLANE[i]))
+EARLY = sum(offset[0] != 2 for offset in PLANE)
 
 
 class Place:
@@ -46,8 +52,14 @@
     def plane_chip(self, offset):
         return lax.rem(self.y + offset[0], 4) * 4 + lax.rem(self.z + offset[1], 4)
 
-    def plane_source(self, offset):
-        return lax.rem(self.y + 4 - offset[0], 4) * 4 + lax.rem(self.z + 4 - offset[1], 4)
+    def slot_to(self, offset):
+        return POSITION[offset[0]] * 4 + lax.rem(self.z + offset[1], 4)
+
+    def slot_from(self, offset):
+        return POSITION[(4 - offset[0]) % 4] * 4 + lax.rem(self.z + 4 - offset[1], 4)
+
+    def landing(self, offset):
+        return POSITION[(4 - offset[0]) % 4] * 4 + self.z
 
     def in_column(self, offset):
         return {"mp": lax.rem(self.x + offset[0], 4), "c": lax.rem(self.c + offset[1], 2)}
@@ -63,6 +75,16 @@
         pl.semaphore_wait(pltpu.get_barrier_semaphore(), len(PLANE) + len(COLUMN))
 
 
+def statistic_tiles():
+    y, c = lax.axis_index("y"), lax.axis_index("c")
+    starts = [((1 - c) * lax.rem(y + ORDER[p], 4) + c * p) * TILE for p in range(NT)]
+    windows = [pl.ds(pl.multiple_of(start, TILE), TILE) for start in starts]
+    for p in range(NT):
+        for q in range(NT):
+            kept = (slice(p * TILE, (p + 1) * TILE), slice(q * TILE, (q + 1) * TILE))
+            yield p * NT + q, kept, (windows[p], windows[q])
+
+
 def remote(src, dst, send, recv, device):
     return pltpu.make_async_remote_copy(
         src_ref=src, dst_ref=dst, send_sem=send, recv_sem=recv, device_id=device, device_id_type=MESH
@@ -102,15 +124,14 @@
 
 
 def gather_kernel(
-    grads, accum, statistic, whole, clip_out, accum_new, graft_out, statistic_out,
+    grads, accum, statistic, whole, clip_out, accum_new, graft_out, statistic_out, gram,
     own, accum_in, tile1, slots1, tile2, slots2,
-    load_sem, bulk_sem, pass_sem, plane_sem, column_sem,
+    load_sem, tile_sem, bulk_sem, pass_sem, plane_sem, column_sem,
 ):
     place = Place()
     load_grads = pltpu.make_async_copy(grads, own, load_sem.at[0])
     load_accum = pltpu.make_async_copy(accum, accum_in, load_sem.at[1])
     load_grads.start()
-    load_statistic = pltpu.make_async_copy(statistic, statistic_out, load_sem.at[2])
     place.greet()
     load_grads.wait()
     squares = jnp.zeros((8, B), F32)
@@ -119,27 +140,44 @@
         squares += (wide * wide).reshape(-1, 8, B).sum(0)
     tile1[...] = to_tile(squares)
     load_accum.start()
-    load_statistic.start()
+    load_tiles = started(
+        [
+            pltpu.make_async_copy(statistic.at[theirs], statistic_out.at[kept], tile_sem.at[i])
+            for i, kept, theirs in statistic_tiles()
+        ]
+    )
     place.met()
     plane = started(plane_sends(place, tile1, slots1, plane_sem))
-    bulk = started(
-        [
-            remote(
-                own.at[place.plane_chip(offset)], whole.at[place.chip, place.c],
-                bulk_sem.at[0, i], bulk_sem.at[1, i], place.plane(offset),
-            )
-            for i, offset in enumerate(PLANE)
-        ]
-    )
+    bulk = [
+        remote(
+            own.at[place.plane_chip(offset)], whole.at[place.landing(offset), place.c],
+            bulk_sem.at[0, i], bulk_sem.at[1, i], place.plane(offset),
+        )
+        for i, offset in enumerate(PLANE)
+    ]
+    started([bulk[i] for i in SEND])
+
+    def pass_on(i):
+        bulk[i].wait_recv()
+        slot = place.slot_from(PLANE[i])
+        return started(
+            [
+                remote(
+                    whole.at[slot, place.c], whole.at[slot, place.c],
+                    pass_sem.at[0, i], pass_sem.at[1, i], place.partner,
+                )
+            ]
+        )
+
     passed = started(
         [
             remote(
-                own.at[place.chip], whole.at[place.chip, place.c],
+                own.at[place.chip], whole.at[place.z, place.c],
                 pass_sem.at[0, 15], pass_sem.at[1, 15], place.partner,
             )
         ]
     )
-    whole[place.chip, place.c] = own[place.chip]
+    whole[place.z, place.c] = own[place.chip]
     tile2[...] = gathered(plane, tile1, slots1, place.chip)
     column = started(column_sends(place, tile2, slots2, column_sem))
     load_accum.wait()
@@ -148,28 +186,44 @@
     clip_out[...] = jnp.broadcast_to(clip, (8, 128))
     graft = jnp.zeros((8, B), F32)
     for i in range(CHIPS):
-        if i < 15:
-            bulk[i].wait_recv()
-            source = place.plane_source(PLANE[i])
-            passed += started(
-                [
-                    remote(
-                        whole.at[source, place.c], whole.at[source, place.c],
-                        pass_sem.at[0, i], pass_sem.at[1, i], place.partner,
-                    )
-                ]
-            )
+        if i < EARLY:
+            passed += pass_on(i)
         scaled = clip * own[i].astype(F32)
         square = scaled * scaled
         accumulated = accum_in[i] + square
         accum_new[i] = accumulated
         graft += (square / accumulated).reshape(-1, 8, B).sum(0)
     graft_out[...] = to_tile(graft)
-    load_statistic.wait()
+    for i in range(EARLY, len(PLANE)):
+        passed += pass_on(i)
+    for copy in passed[: EARLY + 1]:
+        copy.wait_recv()
+    early_gram(place.c, whole, gram)
+    for copy in load_tiles:
+        copy.wait()
     for copy in bulk:
         copy.wait_send()
-    for copy in passed:
+    for copy in passed[: EARLY + 1]:
+        copy.wait_send()
+    for copy in passed[EARLY + 1 :]:
         copy.wait()
+
+
+def early_gram(core, whole, gram):
+    known = (NT - 1) * TILE
+
+    @pl.when(core == 0)
+    def _():
+        rows = whole[:12].reshape(known, B)
+        for j in range(NT - 1):
+            part = rows[j * TILE :]
+            gram[j * TILE : (j + 1) * TILE, j * TILE : known] = dot(part[:TILE], part, 1, 1)
+
+    @pl.when(core == 1)
+    def _():
+        for rows, upper, _ in panels():
+            left = whole[:12, :, :, rows].reshape(known, TILE)
+            gram[rows, upper] = dot(left, whole[:12, :, :, upper].reshape(known, -1), 0, 0)
 
 
 def gather(grads, accum, statistic):
@@ -182,9 +236,10 @@
             jax.ShapeDtypeStruct((CHIPS, ROWS, B), F32),
             jax.ShapeDtypeStruct((8, 128), F32),
             jax.ShapeDtypeStruct((B, B), F32),
+            jax.ShapeDtypeStruct((B, B), F32),
         ),
         in_specs=[HBM, HBM, HBM],
-        out_specs=(VMEM, VMEM, VMEM, VMEM, VMEM),
+        out_specs=(VMEM, VMEM, VMEM, VMEM, VMEM, VMEM),
         scratch_shapes=[
             pltpu.VMEM((CHIPS, ROWS, B), BF16),
             pltpu.VMEM((CHIPS, ROWS, B), F32),
@@ -192,7 +247,8 @@
             pltpu.VMEM((CHIPS, 8, 128), F32),
             pltpu.VMEM((8, 128), F32),
             pltpu.VMEM((8, 8, 128), F32),
-            pltpu.SemaphoreType.DMA((3,)),
+            pltpu.SemaphoreType.DMA((2,)),
+            pltpu.SemaphoreType.DMA((NT * NT,)),
             pltpu.SemaphoreType.DMA((2, 15)),
             pltpu.SemaphoreType.DMA((2, 16)),
             pltpu.SemaphoreType.DMA((2, 15)),
@@ -251,37 +307,53 @@
 
 
 def roots_kernel(
-    whole, clip_in, old, accum_in, statistic_new, root_a, factor, matrix_out, accum_new,
-    new, matrix, square, fourth, sems,
+    whole, gram, clip_in, old, accum_in, statistic_new, root_a, factor, matrix_out, accum_new,
+    new, matrix, square, fourth, norm, accum_sem, tile_sem,
 ):
     core = lax.axis_index("c")
-    put_accum = pltpu.make_async_copy(accum_in, accum_new, sems.at[0])
+    put_accum = pltpu.make_async_copy(accum_in, accum_new, accum_sem)
     put_accum.start()
+    known = (NT - 1) * TILE
+
+    clip = clip_in[0:1, 0:1]
+    weight = 0.1 / B * clip * clip
+
+    def update(products):
+        frob = jnp.zeros((8, 128), F32)
+        for (rows, upper, lower), product in zip(panels(), products):
+            product = product * weight
+            value = 0.9 * old[rows, upper] + product
+            new[rows, upper] = value
+            frob += to_tile(value * value)
+            if lower.start < B:
+                value = 0.9 * old[lower, rows] + product[:, TILE:].T
+                new[lower, rows] = value
+                frob += to_tile(value * value)
+        norm[...] = frob
 
     @pl.when(core == 0)
     def _():
-        for rows, upper, _ in panels():
-            new[rows, upper] = dot(whole[rows, :], whole[upper, :], 1, 1)
+        last = dot(whole[...], whole[known:, :], 1, 1)
+        parts = [
+            jnp.concatenate([gram[rows, upper.start : known], last[rows]], axis=1)
+            for rows, upper, _ in list(panels())[: NT - 1]
+        ]
+        update(parts + [last[known:]])
 
     @pl.when(core == 1)
     def _():
-        for rows, upper, _ in panels():
-            new[rows, upper] = dot(whole[:, rows], whole[:, upper], 0, 0)
-
-    clip = clip_in[0:1, 0:1]
-    weight = 0.1 / B * clip * clip
-    frob = jnp.zeros((8, 128), F32)
-    for rows, upper, lower in panels():
-        gram = new[rows, upper] * weight
-        value = 0.9 * old[rows, upper] + gram
-        new[rows, upper] = value
-        frob += to_tile(value * value)
-        if lower.start < B:
-            value = 0.9 * old[lower, rows] + gram[:, TILE:].T
-            new[lower, rows] = value
-            frob += to_tile(value * value)
-    put_new = pltpu.make_async_copy(new, statistic_new, sems.at[1])
-    put_new.start()
+        update(
+            dot(whole[known:, rows], whole[known:, upper], 0, 0) + gram[rows, upper]
+            for rows, upper, _ in panels()
+        )
+
+    frob = norm[...]
+    put_tiles = started(
+        [
+            pltpu.make_async_copy(new.at[kept], statistic_new.at[theirs], tile_sem.at[i])
+            for i, kept, theirs in statistic_tiles()
+        ]
+    )
     total = jnp.sum(frob, axis=(0, 1), keepdims=True)
     scale = 2.5 / jnp.sqrt(total + 1e-06)
     start = jnp.sqrt(jnp.sqrt(scale)).astype(BF16).astype(F32)
@@ -301,10 +373,11 @@
     symmetric_product(square, square, mirrored_store(fourth))
     symmetric_product(fourth, matrix, factor_store(factor, matrix_out))
     put_accum.wait()
-    put_new.wait()
-
-
-def roots(whole, clip, statistic, accum):
+    for copy in put_tiles:
+        copy.wait()
+
+
+def roots(whole, gram, clip, statistic, accum):
     return pl.pallas_call(
         roots_kernel,
         name="roots",
@@ -315,13 +388,14 @@
             jax.ShapeDtypeStruct((B, B), BF16),
             jax.ShapeDtypeStruct((CHIPS, ROWS, B), F32),
         ),
-        in_specs=[VMEM, VMEM, VMEM, VMEM],
+        in_specs=[VMEM, VMEM, VMEM, VMEM, VMEM],
         out_specs=(HBM, VMEM, VMEM, VMEM, HBM),
         scratch_shapes=[pltpu.VMEM((B, B), F32)]
         + [pltpu.VMEM((B, B), BF16)] * 3
-        + [pltpu.SemaphoreType.DMA((2,))],
+        + [pltpu.VMEM((8, 128), F32)]
+        + [pltpu.SemaphoreType.DMA, pltpu.SemaphoreType.DMA((NT * NT,))],
         compiler_params=pltpu.CompilerParams(vmem_limit_bytes=32 << 20),
-    )(whole, clip, statistic, accum)
+    )(whole, gram, clip, statistic, accum)
 
 
 def apply_kernel(
@@ -347,7 +421,7 @@
 
     def give_back(j, i):
         return remote(
-            product.at[j, place.plane_chip(PLANE[i])], back.at[j, place.chip],
+            product.at[j, place.slot_to(PLANE[i])], back.at[j, place.chip],
             bulk_sem.at[0, j, i], bulk_sem.at[1, j, i], place.plane(PLANE[i]),
         )
 
@@ -405,9 +479,9 @@
             tile1[8:16] = graft[...]
             plane = started(plane_sends(place, tile1, slots1, plane_sem))
         for panel in {0: [0], NT - 1: range(1, NT)}.get(j, []):
-            for i in range(len(PLANE)):
+            for i in RETURN:
                 give_back(panel, i).start()
-        back[j, place.chip] = product[j, place.chip]
+        back[j, place.chip] = product[j, place.z]
 
     tile2[...] = gathered(plane, tile1, slots1, place.chip)
     column = started(column_sends(place, tile2, slots2, column_sem))
@@ -492,11 +566,11 @@
         pltpu.with_memory_space_constraint, memory_space=pltpu.MemorySpace.HBM
     )
     grads = gradients.reshape(CHIPS, ROWS, B)
-    whole, clip, accum, graft, statistic = gather(
+    whole, clip, accum, graft, statistic, gram = gather(
         in_hbm(grads), in_hbm(accumulator.reshape(CHIPS, ROWS, B)), in_hbm(statistics.reshape(B, B))
     )
     whole = whole.reshape(B, B)
-    statistic_new, root, factor, matrix, accum_new = roots(whole, clip, statistic, accum)
+    statistic_new, root, factor, matrix, accum_new = roots(whole, gram, clip, statistic, accum)
     update = scale(*apply(root, factor, matrix, whole, graft))
     return (
         update.reshape(gradients.shape),

time: 65.2 us -> 63.3 us (0.971)
  Pallas kernels: 64.3 us -> 62.4 us
    pallas_call x1, Pallas kernels: 8.63 us -> 7.57 us  [roots(): pl.pallas_call(roots_kernel, name='roots', out_shape=(jax.ShapeDtypeStruc...]
    pallas_call x1, Pallas kernels: 28.3 us -> 27.3 us  [apply(): pl.pallas_call(apply_kernel, name='apply', out_shape=(jax.ShapeDtypeStruc...]
where the time goes in v4:
time: 63.3 us; the launch traced here: 63.2 us
  Pallas kernels  62.4 us (99%)
  between operations  0.81 us (1%)
    pallas_call x1, Pallas kernels, apply(): pl.pallas_call(apply_kernel, name='apply', out_shape=(jax.ShapeDtypeStruc...  27.3 us
    pallas_call x1, Pallas kernels, gather(): pl.pallas_call(gather_kernel, name='gather', out_shape=(jax.ShapeDtypeStr...  26.1 us
    pallas_call x1, Pallas kernels, roots(): pl.pallas_call(roots_kernel, name='roots', out_shape=(jax.ShapeDtypeStruc...  7.57 us
    pallas_call x1, Pallas kernels, scale(): pl.pallas_call(scale_kernel, name='scale', out_shape=jax.ShapeDtypeStruct...  1.42 us

profile of v4, /device:TPU:1, one launch (start us, length us, event | category | flops | bytes accessed | tf_op | source)
XLA Modules:
  0.0 63.2 jit_solution(6694472874603999218)
XLA Ops:
  0.6 26.1 %gather.1 = (bf16[16,2,32,1024]{3,2,1,0:T(8,128)(2,1)S(1)}, f32[8,128]{1,0:T(8,128)S(1)}, f32[16,32,1024]{2,1,0:T(8,128)S(1)}, f32[8,128]{1,0:T(8,128)S(1)}, f32...) custom-call(bf16[16,32,1024]{2,1,0:T(8,128)(2,1)} %bitcast.12, f32[16,32,1024]{2,1,0:T(8,128)} %bitcast.10, ...), custom_call_target="tpu_custom_call" | custom-call | tf_op jit(solution)/shard_map/gather/pallas_call | solution.py:230
  26.7 7.6 %roots.1 = (f32[1024,1024]{1,0:T(8,128)}, bf16[1024,1024]{1,0:T(8,128)(2,1)S(1)}, bf16[1024,1024]{1,0:T(8,128)(2,1)S(1)}, bf16[1024,1024]{1,0:T(8,128)(2,1)S(1)}, f32[16,32,1024]{2,1,0:T(8,128)}) custom-call(bf16[1024,1024]{1,0:T(8,128)(2,1)S(1)} %bitcast.7, f32[1024,1024]{1,0:T(8,128)S(1)} %get-tuple-element.17.gram, ...), custom_call_target="tpu_custom_call" | custom-call | tf_op jit(solution)/shard_map/roots/pallas_call | solution.py:381
  34.3 27.3 %apply.1 = (bf16[4,16,32,256]{3,2,1,0:T(8,128)(2,1)S(1)}, f32[8,128]{1,0:T(8,128)S(1)}) custom-call(bf16[1024,1024]{1,0:T(8,128)(2,1)S(1)} %get-tuple-element.21.root_a, bf16[1024,1024]{1,0:T(8,128)(2,1)S(1)} %get-tuple-element.22.factor_a, bf16[1024,1024]{1,0:T(8,128)(2,1)S(1)} %get-tuple-element.23.matrix, bf16[1024,1024]{1,0:T(8,128)(2,1)S(1)} %bitcast.8, ...), custom_call_target="tpu_custom_call" | custom-call | tf_op jit(solution)/shard_map/apply/pallas_call | solution.py:509
  61.6 1.4 %scale.1 = f32[16,32,1024]{2,1,0:T(8,128)} custom-call(bf16[4,16,32,256]{3,2,1,0:T(8,128)(2,1)S(1)} %get-tuple-element.25.back, f32[8,128]{1,0:T(8,128)S(1)} %get-tuple-element.26.ratio), custom_call_target="tpu_custom_call" | custom-call | tf_op jit(solution)/shard_map/scale/pallas_call | solution.py:553

commit v5 on v4

--- a/solution.py
+++ b/solution.py
@@ -286,9 +286,13 @@
 
 
 def plus_diagonal(value, scale):
-    row = lax.broadcasted_iota(jnp.int32, value.shape, 0)
-    col = lax.broadcasted_iota(jnp.int32, value.shape, 1)
-    return jnp.where(row == col, 1.25, 0.0) - scale * value
+    square = value[:, :TILE]
+    row = lax.broadcasted_iota(jnp.int32, square.shape, 0)
+    col = lax.broadcasted_iota(jnp.int32, square.shape, 1)
+    square = jnp.where(row == col, 1.25 - scale * square, -scale * square)
+    if value.shape[1] == TILE:
+        return square
+    return jnp.concatenate([square, -scale * value[:, TILE:]], axis=1)
 
 
 def factor_store(factor_out, matrix_out):
@@ -356,18 +360,31 @@
     )
     total = jnp.sum(frob, axis=(0, 1), keepdims=True)
     scale = 2.5 / jnp.sqrt(total + 1e-06)
-    start = jnp.sqrt(jnp.sqrt(scale)).astype(BF16).astype(F32)
-
-    @pl.loop(0, B // ROWS)
-    def _(i):
-        rows = pl.ds(pl.multiple_of(i * ROWS, ROWS), ROWS)
-        value = scale * new[rows, :]
-        matrix[rows, :] = value.astype(BF16)
-        row = lax.broadcasted_iota(jnp.int32, value.shape, 0) + i * ROWS
-        col = lax.broadcasted_iota(jnp.int32, value.shape, 1)
-        step = (jnp.where(row == col, 1.25, 0.0) - 0.25 * value).astype(BF16)
-        factor[rows, :] = step
-        root_a[rows, :] = (start * step.astype(F32)).astype(BF16)
+    start = jnp.sqrt(jnp.sqrt(scale)).astype(BF16)
+
+    def first_step(rows, cols, diagonal):
+        value = scale * new[rows, cols]
+        matrix[rows, cols] = value.astype(BF16)
+        step = -0.25 * value
+        if diagonal is not None:
+            row = lax.broadcasted_iota(jnp.int32, value.shape, 0) + diagonal
+            col = lax.broadcasted_iota(jnp.int32, value.shape, 1)
+            step = jnp.where(row == col, 1.25 + step, step)
+        step = step.astype(BF16)
+        factor[rows, cols] = step
+        root_a[rows, cols] = start * step
+
+    for block in range(NT):
+        inside = slice(block * TILE, (block + 1) * TILE)
+
+        @pl.loop(0, TILE // ROWS)
+        def _(i, block=block, inside=inside):
+            rows = pl.ds(pl.multiple_of(block * TILE + i * ROWS, ROWS), ROWS)
+            first_step(rows, inside, i * ROWS)
+            if block:
+                first_step(rows, slice(0, inside.start), None)
+            if block < NT - 1:
+                first_step(rows, slice(inside.stop, B), None)
 
     symmetric_product(factor, factor, mirrored_store(square))
     symmetric_product(square, square, mirrored_store(fourth))
@@ -461,12 +478,12 @@
     squares = jnp.zeros((8, 128), F32)
     for j, (rows, upper, _) in enumerate(panels()):
 
-        if j == 0:
+        if j % 2 == 0:
 
             @pl.when(place.c == 0)
-            def _():
-                for i in range(NT):
-                    swap_right(i).wait_recv()
+            def _(j=j):
+                swap_right(j).wait_recv()
+                swap_right(j + 1).wait_recv()
 
         right_rows = both[1, 4 * j : 4 * j + 4, :, :, upper].reshape(TILE, -1)
         value = dot(applied[:, upper], right_rows, 1, 1)

time: 63.3 us -> 62.9 us (level)
  no operation moved by 1% of the time
where the time goes in v5:
time: 62.9 us; the launch traced here: 62.7 us
  Pallas kernels  61.9 us (98%)
  between operations  0.81 us (1%)
    pallas_call x1, Pallas kernels, apply(): pl.pallas_call(apply_kernel, name='apply', out_shape=(jax.ShapeDtypeStruc...  27.4 us
    pallas_call x1, Pallas kernels, gather(): pl.pallas_call(gather_kernel, name='gather', out_shape=(jax.ShapeDtypeStr...  26.1 us
    pallas_call x1, Pallas kernels, roots(): pl.pallas_call(roots_kernel, name='roots', out_shape=(jax.ShapeDtypeStruc...  7.01 us
    pallas_call x1, Pallas kernels, scale(): pl.pallas_call(scale_kernel, name='scale', out_shape=jax.ShapeDtypeStruct...  1.42 us

profile of v5, /device:TPU:1, one launch (start us, length us, event | category | flops | bytes accessed | tf_op | source)
XLA Modules:
  0.0 62.7 jit_solution(7145882948339235139)
XLA Ops:
  0.6 26.1 %gather.1 = (bf16[16,2,32,1024]{3,2,1,0:T(8,128)(2,1)S(1)}, f32[8,128]{1,0:T(8,128)S(1)}, f32[16,32,1024]{2,1,0:T(8,128)S(1)}, f32[8,128]{1,0:T(8,128)S(1)}, f32...) custom-call(bf16[16,32,1024]{2,1,0:T(8,128)(2,1)} %bitcast.12, f32[16,32,1024]{2,1,0:T(8,128)} %bitcast.10, ...), custom_call_target="tpu_custom_call" | custom-call | tf_op jit(solution)/shard_map/gather/pallas_call | solution.py:230
  26.7 7.0 %roots.1 = (f32[1024,1024]{1,0:T(8,128)}, bf16[1024,1024]{1,0:T(8,128)(2,1)S(1)}, bf16[1024,1024]{1,0:T(8,128)(2,1)S(1)}, bf16[1024,1024]{1,0:T(8,128)(2,1)S(1)}, f32[16,32,1024]{2,1,0:T(8,128)}) custom-call(bf16[1024,1024]{1,0:T(8,128)(2,1)S(1)} %bitcast.7, f32[1024,1024]{1,0:T(8,128)S(1)} %get-tuple-element.17.gram, ...), custom_call_target="tpu_custom_call" | custom-call | tf_op jit(solution)/shard_map/roots/pallas_call | solution.py:398
  33.7 27.4 %apply.1 = (bf16[4,16,32,256]{3,2,1,0:T(8,128)(2,1)S(1)}, f32[8,128]{1,0:T(8,128)S(1)}) custom-call(bf16[1024,1024]{1,0:T(8,128)(2,1)S(1)} %get-tuple-element.21.root_a, bf16[1024,1024]{1,0:T(8,128)(2,1)S(1)} %get-tuple-element.22.factor_a, bf16[1024,1024]{1,0:T(8,128)(2,1)S(1)} %get-tuple-element.23.matrix, bf16[1024,1024]{1,0:T(8,128)(2,1)S(1)} %bitcast.8, ...), custom_call_target="tpu_custom_call" | custom-call | tf_op jit(solution)/shard_map/apply/pallas_call | solution.py:526
  61.2 1.4 %scale.1 = f32[16,32,1024]{2,1,0:T(8,128)} custom-call(bf16[4,16,32,256]{3,2,1,0:T(8,128)(2,1)S(1)} %get-tuple-element.25.back, f32[8,128]{1,0:T(8,128)S(1)} %get-tuple-element.26.ratio), custom_call_target="tpu_custom_call" | custom-call | tf_op jit(solution)/shard_map/scale/pallas_call | solution.py:570
